TPU v7x, 256 devices: a whole 4x4x8 slice. The times are simulated.
256 devices in a mesh: row: 8 (over x, core), col: 32 (over z, y).
Axes of the slice: x: 4, y: 4, z: 8, core: 2. Of those that a mesh axis runs over, the one named last changes fastest.
Arguments:
- diag_block: float32 [512, 512], P(None, 'col'), may hold values from -0.2 to 2, as said below
- panel_below: float32 [16384, 512], P('col', 'row'), may hold values from -0.26516503 to 0.26516503
- trail_inverse: float32 [16384, 16384], P('row', 'col'), may hold values from -0.046875 to 0.046875
Outputs:
- inverse_panel: float32 [16384, 512], P('row', 'col')
- product_panel: float32 [16384, 512], P('col', 'row')
Inputs may be any that keep to these rules, and one draw needn't show every extreme that they name: diag_block is lower triangular with diagonal entries between 1 and 2 and off-diagonal entries of magnitude at most 0.2.
All inputs are finite; a program needn't handle non-finite values.
Results may differ from a plain program's by a relative error of at most 0.000094.
Values sent between devices are 32-bit elements; how exact they have to be, the bound alone decides.
No kernel may reach another device: no remote copies, remote signals or barrier semaphores. Data moves between devices by JAX's collectives and lax.ppermute only.
A program may use at most 64 MiB of HBM per device.

v0:
```python
import functools

import jax
import jax.numpy as jnp
from jax import lax
from jax.experimental import pallas as pl
from jax.experimental.pallas import tpu as pltpu
from jax.sharding import Mesh
from jax.sharding import PartitionSpec as P


ROW = ("x", "core")
COL = ("z", "y")
NX, NC, NZ, NY = 4, 2, 8, 4
NR, NCOL = NX * NC, NZ * NY
BLK = 512
ROWS = 2048
PIECE = ROWS // NCOL
CHUNK = NZ * PIECE
WIDTH = 4
TILE = 128
STEP = 256

ORDER = (2, 1, 3, 0)
OFFSET = {dy: CHUNK * place for place, dy in enumerate(ORDER)}


VMEM = pl.BlockSpec(memory_space=pltpu.VMEM)
SMEM = pl.BlockSpec(memory_space=pltpu.SMEM)
NT = (((1,), (1,)), ((), ()))
TN = (((0,), (0,)), ((), ()))
NN = (((1,), (0,)), ((), ()))


def call(kernel, out, n_in, flops=0, scratch=(), smem=True, mib=8):
    many = isinstance(out, (list, tuple))
    return pl.pallas_call(
        kernel,
        out_shape=out,
        in_specs=([SMEM] if smem else []) + [VMEM] * n_in,
        out_specs=[VMEM] * len(out) if many else VMEM,
        scratch_shapes=list(scratch),
        compiler_params=pltpu.CompilerParams(vmem_limit_bytes=mib << 20),
        cost_estimate=pl.CostEstimate(flops=flops, bytes_accessed=1 << 20, transcendentals=0),
    )


def halves(value):
    high = value.astype(jnp.bfloat16)
    low = (value - high.astype(jnp.float32)).astype(jnp.bfloat16)
    return high, low


def dot_full(a, b, dims=NN):
    return lax.dot_general(
        a, b, dims, precision=lax.Precision.HIGHEST, preferred_element_type=jnp.float32
    )


def prepare_kernel(idx, w, out):
    x, core, z, y = idx[0], idx[1], idx[2], idx[3]
    shift = (x * NC + core) - (z * NY + y)

    def piece(source, target, size):
        source = pl.multiple_of(source, size)
        target = pl.multiple_of(target, size)
        delta = (source >> 9) * NR + shift
        rows = pl.ds(source, size)
        place = pl.ds(target, size)

        @pl.when(delta > 0)
        def _():
            out[place, :] = w[rows, :]

        @pl.when(delta < 0)
        def _():
            out[place, :] = jnp.zeros((size, BLK), jnp.float32)

        @pl.when(delta == 0)
        def _():
            row = lax.broadcasted_iota(jnp.int32, (size, BLK), 0) + (source & (BLK - 1))
            col = lax.broadcasted_iota(jnp.int32, (size, BLK), 1)
            lower = jnp.where(row >= col, w[rows, :], 0.0)
            out[place, :] = lower + jnp.where(row == col, 1.0, 0.0)

    for dy, offset in OFFSET.items():
        owner_y = lax.rem(y + dy, NY)

        @pl.loop(0, NZ)
        def _(dz):
            owner_z = lax.rem(z + dz, NZ)
            piece(owner_y * CHUNK + owner_z * PIECE, offset + dz * PIECE, PIECE)


def merge(a, b):
    return dot_three(halves(a), halves(b), NN)


def place(t, extent=TILE):
    return pl.ds(pl.multiple_of(t * TILE, TILE), extent)


def tiles_kernel(idx, mine, other, u, work):
    core = idx[1]
    size = TILE
    tiles = BLK // size
    half = BLK // 2
    u[:, pl.ds(pl.multiple_of(core * half, half), half)] = mine[...]
    u[:, pl.ds(pl.multiple_of((1 - core) * half, half), half)] = other[...]
    work[...] = jnp.zeros_like(work)
    row = lax.broadcasted_iota(jnp.int32, (size, size), 0)
    col = lax.broadcasted_iota(jnp.int32, (size, size), 1)
    eye = jnp.where(row == col, 1.0, 0.0)

    @pl.loop(0, tiles // WIDTH)
    def _(k):
        spots = [place(WIDTH * k + t) for t in range(WIDTH)]
        parts = [u[spot, spot] for spot in spots]
        diagonals = [jnp.where(row == col, v, 0.0) for v in parts]
        upper = [
            jnp.where(row < col, v, 0.0) / jnp.sum(d, axis=1, keepdims=True)
            for v, d in zip(parts, diagonals)
        ]
        base = 16
        power = [jnp.where((row // base) == (col // base), n, 0.0) for n in upper]
        inv = [eye - n for n in power]
        for _ in range(3):
            power = [dot_full(n, n) for n in power]
            inv = [v + dot_full(v, n) for v, n in zip(inv, power)]
        while base < size:
            pair = ((row // (2 * base)) == (col // (2 * base))) & ((row // base) != (col // base))
            edge = [jnp.where(pair, n, 0.0) for n in upper]
            inv = [v - merge(merge(v, e), v) for v, e in zip(inv, edge)]
            base *= 2
        for spot, v, d in zip(spots, inv, diagonals):
            work[spot, spot] = v / jnp.sum(d, axis=0, keepdims=True)


def inverse_kernel(idx, u, diagonal, out, work, left):
    x, core = idx[0], idx[1]
    tiles = BLK // TILE
    half = BLK // 2
    work[...] = diagonal[...]

    @pl.loop(0, tiles // 2)
    def _(k):
        a, b = place(2 * k), place(2 * k + 1)
        work[a, b] = -merge(merge(work[a, a], u[a, b]), work[b, b])

    @pl.loop(0, 2)
    def _(k):
        left[:, place(k)] = merge(work[:half, :half], u[:half, place(k + 2)])

    @pl.loop(0, 2)
    def _(k):
        work[:half, place(k + 2)] = -merge(left[...], work[half:, place(k + 2)])

    @pl.loop(0, tiles * tiles)
    def _(k):
        r, c = k >> 2, k & 3
        block = pltpu.roll(pltpu.roll(work[place(c), place(r)].T, core * 64, 0), core * 64, 1)
        out[place((r - x + tiles) & 3), place((c - x + tiles) & 3)] = block


def halves(value):
    high = value.astype(jnp.bfloat16)
    return high, (value - high.astype(jnp.float32)).astype(jnp.bfloat16)


def dot_three(a, b, dims):
    terms = [
        lax.dot_general(u, v, dims, preferred_element_type=jnp.float32)
        for u, v in ((a[0], b[1]), (a[1], b[0]), (a[0], b[0]))
    ]
    return (terms[0] + terms[1]) + terms[2]


def product_kernel(first, panel, w, *refs):
    outs, high, low = refs[:-2], refs[-2], refs[-1]
    high[...], low[...] = halves(panel[...])
    for out in outs:

        @pl.loop(0, out.shape[0] // STEP)
        def _(i):
            rows = pl.ds(pl.multiple_of(first + i * STEP, STEP), STEP)
            target = pl.ds(pl.multiple_of(i * STEP, STEP), STEP)
            out[target, :] = dot_three(halves(w[rows, :]), (high[...], low[...]), NT)

        first += out.shape[0]


def near_kernel(w, *refs):
    chunks, out = refs[:3], refs[3]
    out[...] = jnp.zeros_like(out)
    for k, chunk in enumerate(chunks):

        @pl.loop(0, CHUNK // STEP)
        def _(i):
            rows = pl.ds(pl.multiple_of(CHUNK * (k + 1) + i * STEP, STEP), STEP)
            source = pl.ds(pl.multiple_of(i * STEP, STEP), STEP)
            out[...] += dot_three(halves(chunk[source, :]), halves(w[rows, :]), TN)


def scale_kernel(x11, a0, a1, a2, out):
    out[...] = -dot_full(a0[...] + a1[...] + a2[...], x11[...])


def columns_kernel(idx, far_low, far_up, up, down, own, out, held):
    x, core, z, y = idx[0], idx[1], idx[2], idx[3]
    column = z * NY + y
    tile = lax.rem((column >> 3) - x + NX, NX)
    inside = ((((column >> 2) & 1) + core) & 1) * 64 + (column & 3) * 16
    lanes = pl.ds(pl.multiple_of(tile * 128, 128), 128)
    turn = lax.rem(128 - inside, 128)
    half = CHUNK // 2
    for dy, source, first, size in (
        (2, far_low, 0, half), (2, far_up, half, half), (1, up, 0, CHUNK), (3, down, 0, CHUNK), (0, own, 0, CHUNK)
    ):
        owner_y = lax.rem(y + dy, NY)

        @pl.loop(0, size // PIECE)
        def _(k):
            owner_z = lax.rem(z + k + first // PIECE, NZ)
            start = pl.multiple_of(k * PIECE, PIECE)
            target = pl.multiple_of(owner_y * CHUNK + owner_z * PIECE, PIECE)
            value = source[pl.ds(start, PIECE), lanes]
            held[pl.ds(target, PIECE), :] = pltpu.roll(value, turn, 1)

    out[...] = held[...].T[:16, :]


def ring(axis):
    n = lax.axis_size(axis)
    right = [(i, (i + 1) % n) for i in range(n)]
    left = [(i, (i - 1) % n) for i in range(n)]
    return n, lambda v: lax.ppermute(v, axis, right), lambda v: lax.ppermute(v, axis, left)


def shifted(value, axis, hops):
    n = lax.axis_size(axis)
    return lax.ppermute(value, axis, [(i, (i + hops) % n) for i in range(n)])


def sum_to_owner(chunks, far, axis):
    n, right, left = ring(axis)
    half = far[0].shape[0]
    a, b = right(far[0]), left(far[1])
    for hop in range(n // 2 - 1, 0, -1):
        a, b = lax.optimization_barrier((a, b))
        if hop == n // 2 - 1:
            a = jnp.pad(a, ((0, half), (0, 0)))
            b = jnp.pad(b, ((half, 0), (0, 0)))
        up, down = chunks[hop] + a, chunks[n - hop] + b
        a, b = right(up), left(down)
    return chunks[0], a, b


def gather(own, axis):
    n, right, left = ring(axis)
    half = own.shape[0] // 2
    chunks = {0: own}
    a = b = own
    for hop in range(1, n // 2):
        a, b = right(a), left(b)
        chunks[n - hop], chunks[hop] = a, b
    return chunks, right(a[:half]), left(b[half:])


def joined(chunks, n, lower, upper):
    parts = []
    for hop in range(n):
        parts += [lower, upper] if hop == n // 2 else [chunks[hop]]
    return jnp.concatenate(parts, axis=0)


def dot_high(a, b, dims):
    return lax.dot_general(
        a, b, dims, precision=lax.Precision.HIGH, preferred_element_type=jnp.float32
    )


def steps(diag_block, panel_below, trail_inverse):
    f32 = jnp.float32
    shape = jax.ShapeDtypeStruct
    idx = jnp.stack([lax.axis_index(a) for a in ("x", "core", "z", "y")]).astype(jnp.int32)
    swap = lambda v: lax.ppermute(v, "core", [(0, 1), (1, 0)])

    own = panel_below.T
    mine = jnp.stack([own, shifted(own, "x", -1), shifted(own, "x", 2), shifted(own, "x", 1)])
    other = swap(mine)
    panel = jnp.stack([mine, other], axis=1).reshape(BLK, BLK)

    half = BLK // NC
    part = lax.dynamic_slice_in_dim(diag_block.T, lax.axis_index("core") * half, half, 1)
    for axis in ("y", "z"):
        copies = jnp.broadcast_to(part, (lax.axis_size(axis), *part.shape))
        part = lax.all_to_all(copies, axis, split_axis=0, concat_axis=0, tiled=True)
        part = part.reshape(-1, half)
    block = part
    across = swap(block)
    square = shape((BLK, BLK), f32)
    u, tiles = call(tiles_kernel, [square] * 2, 2, 10**9)(idx, block, across)
    x11 = call(
        inverse_kernel,
        square,
        2,
        10**9,
        scratch=[pltpu.VMEM((BLK, BLK), f32), pltpu.VMEM((half, half), f32)],
    )(idx, u, tiles)

    w = call(prepare_kernel, shape((ROWS, BLK), f32), 1, 10**8, mib=10)(idx, trail_inverse)

    def product(first, outs):
        rows = sum(out.shape[0] for out in outs)
        return call(
            functools.partial(product_kernel, first),
            outs,
            2,
            6 * rows * BLK * BLK,
            scratch=[pltpu.VMEM((BLK, BLK), jnp.bfloat16)] * 2,
            smem=False,
            mib=14,
        )(panel, w)

    far = product(0, [shape((CHUNK // 2, BLK), f32)] * 2)
    later = product(CHUNK, [shape((CHUNK, BLK), f32)] * 3)
    partial = dict(zip(ORDER[1:], later))

    part = sum(sum_to_owner(partial, far, "y"))
    parts = {d: part[d * PIECE : (d + 1) * PIECE] for d in range(NZ)}
    cut = NZ // 2 * PIECE + PIECE // 2
    far = (part[cut - PIECE // 2 : cut], part[cut : cut + PIECE // 2])
    parts = sum_to_owner(parts, far, "z")
    own = call(scale_kernel, shape((PIECE, BLK), f32), 4, 12 * PIECE * BLK * BLK, smem=False)(x11, *parts)
    own = joined_gather(own, "z")
    chunks, far_low, far_up = gather(own, "y")
    total = call(
        near_kernel, shape((BLK, BLK), f32), 4, 6 * (ROWS - CHUNK) * BLK * BLK, smem=False, mib=14
    )(w, *[chunks[dy] for dy in ORDER[1:]])
    update = total + dot_high(jnp.concatenate([far_low, far_up], axis=0), w[:CHUNK], TN)
    columns = call(
        columns_kernel, shape((16, ROWS), f32), 5, 10**7, scratch=[pltpu.VMEM((ROWS, 128), f32)]
    )(idx, far_low, far_up, chunks[1], chunks[3], own)

    blocks = update.reshape(NX, NC, 64, BLK)
    rows = blocks[:, 0] + swap(blocks[:, 1])
    product = rows[0] + shifted(rows[1], "x", 1) + shifted(rows[3], "x", -1) + shifted(rows[2], "x", 2)
    return columns.T, product.T


def joined_gather(own, axis):
    chunks, lower, upper = gather(own, axis)
    return joined(chunks, lax.axis_size(axis), lower, upper)


def solution(mesh):
    torus = Mesh(mesh.devices.reshape(NX, NC, NZ, NY), ("x", "core", "z", "y"))
    return jax.shard_map(
        steps,
        mesh=torus,
        in_specs=(P(None, COL), P(COL, ROW), P(ROW, COL)),
        out_specs=(P(ROW, COL), P(COL, ROW)),
        check_vma=False,
    )
```

profile of v0, /device:TPU:1, one launch (start us, length us, event | category | flops | bytes accessed | tf_op | source)
XLA Modules:
  0.0 185.6 jit_solution(10337210889163319594)
XLA Ops:
  0.6 3.6 %collective-permute-start.2 = (f32[64,512]{1,0:T(8,128)}, f32[64,512]{1,0:T(8,128)S(1)}, u32[]{:S(2)}, u32[]{:S(2)}) collective-permute-start(f32[64,512]{1,0:T(8,128)} %bitcast.56), channel_id=1, source_target_pairs={{0,128},{64,192},{128,0},{192,64},{1,129},{65,193},{129,1},{193,65... | collective-permute-start | bytes 393224 | tf_op jit(solution)/shard_map/ppermute | solution.py:241
  4.6 2.4 %collective-permute-start.1 = (f32[64,512]{1,0:T(8,128)}, f32[64,512]{1,0:T(8,128)S(1)}, u32[]{:S(2)}, u32[]{:S(2)}) collective-permute-start(f32[64,512]{1,0:T(8,128)} %bitcast.58), channel_id=1, source_target_pairs={{0,192},{64,0},{128,64},{192,128},{1,193},{65,1},{129,65},{193,129... | collective-permute-start | bytes 393224 | tf_op jit(solution)/shard_map/ppermute | solution.py:241
  7.0 4.8 %collective-permute-done.3 = f32[64,512]{1,0:T(8,128)S(1)} collective-permute-done((f32[64,512]{1,0:T(8,128)}, f32[64,512]{1,0:T(8,128)S(1)}, u32[]{:S(2)}, u32[]{:S(2)}) %collective-permute-start.3) | collective-permute-done | bytes 131104 | tf_op jit(solution)/shard_map/ppermute | solution.py:241
  14.2 2.2 %copy-done.3 = f32[2048,512]{1,0:T(8,128)S(1)} copy-done((f32[2048,512]{1,0:T(8,128)S(1)}, f32[2048,512]{1,0:T(8,128)}, u32[]{:S(2)}) %copy-start.3) | copy-done | bytes 4194328
  20.1 2.0 %collective-permute-start.6 = (f32[256,512]{1,0:T(8,128)S(1)}, f32[256,512]{1,0:T(8,128)S(1)}, u32[]{:S(2)}, u32[]{:S(2)}) collective-permute-start(f32[256,512]{1,0:T(8,128)S(1)} %get-tuple-element.22), channel_id=1, source_target_pairs={{0,3},{1,0},{2,1},{3,2},{4,7},{5,4},{6,5},{7,6},{8,11},{9,8},{10,9... | collective-permute-start | bytes 1572872 | tf_op jit(solution)/shard_map/ppermute | solution.py:236
  22.1 3.8 %shard_map.53 = (f32[512,512]{1,0:T(8,128)S(1)}, f32[512,512]{1,0:T(8,128)S(1)}, f32[512,512]{1,0:T(8,128)S(1)}) custom-call(f32[512,512]{1,0:T(8,128)S(1)} %bitcast.49, f32[2048,512]{1,0:T(8,128)S(1)} %shard_map.52.w), custom_call_target="tpu_custom_call" | custom-call | flops 2415919104 | bytes 1048576 | tf_op jit(solution)/shard_map/pallas_call | solution.py:315
  25.8 8.1 %collective-permute-done.5 = f32[256,512]{1,0:T(8,128)S(1)} collective-permute-done((f32[256,512]{1,0:T(8,128)S(1)}, f32[256,512]{1,0:T(8,128)S(1)}, u32[]{:S(2)}, u32[]{:S(2)}) %collective-permute-start.5) | collective-permute-done | bytes 524320 | tf_op jit(solution)/shard_map/ppermute | solution.py:236
  35.8 2.2 %collective-permute-start.8 = (f32[512,512]{1,0:T(8,128)}, f32[512,512]{1,0:T(8,128)}, u32[]{:S(2)}, u32[]{:S(2)}) collective-permute-start(f32[512,512]{1,0:T(8,128)} %pad_add_fusion), channel_id=1, source_target_pairs={{0,3},{1,0},{2,1},{3,2},{4,7},{5,4},{6,5},{7,6},{8,11},{9,8},{10,9... | collective-permute-start | bytes 3145736 | tf_op jit(solution)/shard_map/ppermute | solution.py:236
  37.9 22.1 %all_to_all.10 = f32[4,16,256]{2,1,0:T(8,128)S(1)} all-to-all(f32[4,16,256]{2,1,0:T(8,128)S(1)} %broadcast_in_dim.6), channel_id=1, replica_groups=mesh['x'=4,'core'=2,'z'=8,'y'=4] {'y'}, dimensions={0} | all-to-all | bytes 131072 | tf_op jit(solution)/shard_map/all_to_all | solution.py:297
  61.0 7.9 %all-to-all-start.1 = ((f32[8,64,256]{2,1,0:T(8,128)}), f32[8,64,256]{2,1,0:T(8,128)S(1)}, u32[]{:S(2)}, u32[]{:S(2)}) async-start(f32[8,64,256]{2,1,0:T(8,128)} %broadcast_in_dim.7), calls=%async_computation.1 | async-start | bytes 1048576 | tf_op jit(solution)/shard_map/all_to_all | solution.py:297
  70.8 2.7 %collective-permute-start.10 = (f32[32,512]{1,0:T(8,128)S(1)}, f32[32,512]{1,0:T(8,128)S(1)}, u32[]{:S(2)}, u32[]{:S(2)}) collective-permute-start(f32[32,512]{1,0:T(8,128)S(1)} %get-tuple-element.39), channel_id=1, source_target_pairs={{0,28},{4,0},{8,4},{12,8},{16,12},{20,16},{24,20},{28,24},{1,29},{... | collective-permute-start | bytes 196616 | tf_op jit(solution)/shard_map/ppermute | solution.py:236
  73.5 6.9 %collective-permute-done.10 = f32[32,512]{1,0:T(8,128)S(1)} collective-permute-done((f32[32,512]{1,0:T(8,128)S(1)}, f32[32,512]{1,0:T(8,128)S(1)}, u32[]{:S(2)}, u32[]{:S(2)}) %collective-permute-start.10) | collective-permute-done | bytes 65568 | tf_op jit(solution)/shard_map/ppermute | solution.py:236
  80.4 2.1 %collective-permute-done.9 = f32[32,512]{1,0:T(8,128)S(1)} collective-permute-done((f32[32,512]{1,0:T(8,128)S(1)}, f32[32,512]{1,0:T(8,128)S(1)}, u32[]{:S(2)}, u32[]{:S(2)}) %collective-permute-start.9) | collective-permute-done | bytes 65568 | tf_op jit(solution)/shard_map/ppermute | solution.py:236
  82.7 2.7 %collective-permute-start.12 = (f32[64,512]{1,0:T(8,128)S(1)}, f32[64,512]{1,0:T(8,128)S(1)}, u32[]{:S(2)}, u32[]{:S(2)}) collective-permute-start(f32[64,512]{1,0:T(8,128)S(1)} %get-tuple-element.37), channel_id=1, source_target_pairs={{0,28},{4,0},{8,4},{12,8},{16,12},{20,16},{24,20},{28,24},{1,29},{... | collective-permute-start | bytes 393224 | tf_op jit(solution)/shard_map/ppermute | solution.py:236
  85.3 2.8 %collective-permute-start = (f32[512,256]{1,0:T(8,128)S(1)}, f32[512,256]{1,0:T(8,128)S(1)}, u32[]{:S(2)}, u32[]{:S(2)}) collective-permute-start(f32[512,256]{1,0:T(8,128)S(1)} %bitcast.50), channel_id=1, source_target_pairs={{0,32},{32,0},{1,33},{33,1},{2,34},{34,2},{3,35},{35,3},{4,36},{36... | collective-permute-start | bytes 1572872 | tf_op jit(solution)/shard_map/ppermute | solution.py:286
  88.8 2.1 %collective-permute-start.14 = (f32[64,512]{1,0:T(8,128)S(1)}, f32[64,512]{1,0:T(8,128)S(1)}, u32[]{:S(2)}, u32[]{:S(2)}) collective-permute-start(f32[64,512]{1,0:T(8,128)S(1)} %get-tuple-element.35), channel_id=1, source_target_pairs={{0,28},{4,0},{8,4},{12,8},{16,12},{20,16},{24,20},{28,24},{1,29},{... | collective-permute-start | bytes 393224 | tf_op jit(solution)/shard_map/ppermute | solution.py:236
  90.9 2.4 %collective-permute-done.13 = f32[64,512]{1,0:T(8,128)S(1)} collective-permute-done((f32[64,512]{1,0:T(8,128)S(1)}, f32[64,512]{1,0:T(8,128)S(1)}, u32[]{:S(2)}, u32[]{:S(2)}) %collective-permute-start.13) | collective-permute-done | bytes 131104 | tf_op jit(solution)/shard_map/ppermute | solution.py:236
  93.9 3.0 %collective-permute-start.15 = (f32[64,512]{1,0:T(8,128)S(1)}, f32[64,512]{1,0:T(8,128)S(1)}, u32[]{:S(2)}, u32[]{:S(2)}) collective-permute-start(f32[64,512]{1,0:T(8,128)S(1)} %get-tuple-element.33), channel_id=1, source_target_pairs={{0,4},{4,8},{8,12},{12,16},{16,20},{20,24},{24,28},{28,0},{1,5},{5... | collective-permute-start | bytes 393224 | tf_op jit(solution)/shard_map/ppermute | solution.py:236
  96.9 3.3 %shard_map.50 = (f32[512,512]{1,0:T(8,128)S(1)}, f32[512,512]{1,0:T(8,128)S(1)}) custom-call(s32[4]{0:T(128)S(1)} %pad_add_fusion.2.idx, f32[512,256]{1,0:T(8,128)S(1)} %bitcast.51, f32[512,256]{1,0:T(8,128)S(1)} %collective-permute-done.other), custom_call_target="tpu_custom_call" | custom-call | flops 1000000000 | bytes 1048576 | tf_op jit(solution)/shard_map/pallas_call | solution.py:302
  100.2 5.6 %shard_map.51.x11 = f32[512,512]{1,0:T(8,128)S(1)} custom-call(s32[4]{0:T(128)S(1)} %pad_add_fusion.2.idx, f32[512,512]{1,0:T(8,128)S(1)} %get-tuple-element.17.u, f32[512,512]{1,0:T(8,128)S(1)} %get-tuple-element.18.diagonal), custom_call_target="tpu_custom_call" | custom-call | flops 1000000000 | bytes 1048576 | tf_op jit(solution)/shard_map/pallas_call | solution.py:303
  108.2 2.3 %collective-permute-done.17 = f32[64,512]{1,0:T(8,128)S(1)} collective-permute-done((f32[64,512]{1,0:T(8,128)S(1)}, f32[64,512]{1,0:T(8,128)S(1)}, u32[]{:S(2)}, u32[]{:S(2)}) %collective-permute-start.17) | collective-permute-done | bytes 131104 | tf_op jit(solution)/shard_map/ppermute | solution.py:236
  112.3 2.9 %collective-permute-done.18 = f32[64,512]{1,0:T(8,128)S(1)} collective-permute-done((f32[64,512]{1,0:T(8,128)S(1)}, f32[64,512]{1,0:T(8,128)S(1)}, u32[]{:S(2)}, u32[]{:S(2)}) %collective-permute-start.18) | collective-permute-done | bytes 131104 | tf_op jit(solution)/shard_map/ppermute | solution.py:236
  115.2 3.4 %collective-permute-start.19 = (f32[64,512]{1,0:T(8,128)S(1)}, f32[64,512]{1,0:T(8,128)S(1)}, u32[]{:S(2)}, u32[]{:S(2)}) collective-permute-start(f32[64,512]{1,0:T(8,128)S(1)} %collective-permute-done.18), channel_id=1, source_target_pairs={{0,28},{4,0},{8,4},{12,8},{16,12},{20,16},{24,20},{28,24},{1,29},{... | collective-permute-start | bytes 393224 | tf_op jit(solution)/shard_map/ppermute | solution.py:236
  118.7 5.0 %collective-permute-done.22 = f32[64,512]{1,0:T(8,128)S(1)} collective-permute-done((f32[64,512]{1,0:T(8,128)S(1)}, f32[64,512]{1,0:T(8,128)S(1)}, u32[]{:S(2)}, u32[]{:S(2)}) %collective-permute-start.22) | collective-permute-done | bytes 131104 | tf_op jit(solution)/shard_map/ppermute | solution.py:236
  123.7 2.7 %collective-permute-start.24 = (f32[32,512]{1,0:T(8,128)S(1)}, f32[32,512]{1,0:T(8,128)S(1)}, u32[]{:S(2)}, u32[]{:S(2)}) collective-permute-start(f32[32,512]{1,0:T(8,128)S(1)} %slice.90), channel_id=1, source_target_pairs={{0,28},{4,0},{8,4},{12,8},{16,12},{20,16},{24,20},{28,24},{1,29},{... | collective-permute-start | bytes 196616 | tf_op jit(solution)/shard_map/ppermute | solution.py:236
  131.7 14.1 %collective-permute-done.25.down.refs_1_ = f32[512,512]{1,0:T(8,128)S(1)} collective-permute-done((f32[512,512]{1,0:T(8,128)S(1)}, f32[512,512]{1,0:T(8,128)S(1)}, u32[]{:S(2)}, u32[]{:S(2)}) %collective-permute-start.25) | collective-permute-done | bytes 1048608 | tf_op jit(solution)/shard_map/ppermute | solution.py:236
  145.9 2.7 %collective-permute-start.28 = (f32[256,512]{1,0:T(8,128)S(1)}, f32[256,512]{1,0:T(8,128)S(1)}, u32[]{:S(2)}, u32[]{:S(2)}) collective-permute-start(f32[256,512]{1,0:T(8,128)S(1)} %slice.92), channel_id=1, source_target_pairs={{0,3},{1,0},{2,1},{3,2},{4,7},{5,4},{6,5},{7,6},{8,11},{9,8},{10,9... | collective-permute-start | bytes 1572872 | tf_op jit(solution)/shard_map/ppermute | solution.py:236
  148.7 3.8 %shard_map.57 = f32[512,512]{1,0:T(8,128)S(1)} custom-call(f32[2048,512]{1,0:T(8,128)S(1)} %copy-done.2, f32[512,512]{1,0:T(8,128)S(1)} %collective-permute-done.27.up.refs_0_, f32[512,512]{1,0:T(8,128)S(1)} %collective-permute-done.25.down.refs_1_, f32[512,512]{1,0:T(8,128)S(1)} %constant_dynamic-update-slice_fusion.own.refs_2_), custom_call_target="tpu_custom_call" | custom-call | flops 2415919104 | bytes 1048576 | tf_op jit(solution)/shard_map/pallas_call | solution.py:337
  152.4 8.4 %collective-permute-done.26.far_low = f32[256,512]{1,0:T(8,128)S(1)} collective-permute-done((f32[256,512]{1,0:T(8,128)S(1)}, f32[256,512]{1,0:T(8,128)S(1)}, u32[]{:S(2)}, u32[]{:S(2)}) %collective-permute-start.26) | collective-permute-done | bytes 524320 | tf_op jit(solution)/shard_map/ppermute | solution.py:236
  162.1 11.0 %collective-permute-start.29 = (f32[4,64,512]{2,1,0:T(8,128)S(1)}, f32[4,64,512]{2,1,0:T(8,128)S(1)}, u32[]{:S(2)}, u32[]{:S(2)}) collective-permute-start(f32[4,64,512]{2,1,0:T(8,128)S(1)} %slice_bitcast_fusion), channel_id=1, source_target_pairs={{0,32},{32,0},{1,33},{33,1},{2,34},{34,2},{3,35},{35,3},{4,36},{36... | collective-permute-start | bytes 1572872 | tf_op jit(solution)/shard_map/ppermute | solution.py:286
  178.9 3.9 %shard_map.56 = f32[16,2048]{1,0:T(8,128)} custom-call(s32[4]{0:T(128)S(1)} %pad_add_fusion.2.idx, f32[256,512]{1,0:T(8,128)S(1)} %collective-permute-done.26.far_low, f32[256,512]{1,0:T(8,128)S(1)} %collective-permute-done.28.far_up, f32[512,512]{1,0:T(8,128)S(1)} %collective-permute-done.27.up.refs_0_, ...), custom_call_target="tpu_custom_call" | custom-call | flops 10000000 | bytes 1048576 | tf_op jit(solution)/shard_map/pallas_call | solution.py:341
  182.9 2.1 %collective-permute-done.32 = f32[64,512]{1,0:T(8,128)S(1)} collective-permute-done((f32[64,512]{1,0:T(8,128)S(1)}, f32[64,512]{1,0:T(8,128)S(1)}, u32[]{:S(2)}, u32[]{:S(2)}) %collective-permute-start.32) | collective-permute-done | bytes 131104 | tf_op jit(solution)/shard_map/ppermute | solution.py:241
  (86 shorter events, 29.8 us)
Async XLA Ops:
  0.6 6.3 %collective-permute-start.2 = (f32[64,512]{1,0:T(8,128)}, f32[64,512]{1,0:T(8,128)S(1)}, u32[]{:S(2)}, u32[]{:S(2)}) collective-permute-start(f32[64,512]{1,0:T(8,128)} %bitcast.56), channel_id=1, source_target_pairs={{0,128},{64,192},{128,0},{192,64},{1,129},{65,193},{129,1},{193,65... | collective-permute-start | bytes 393224 | tf_op jit(solution)/shard_map/ppermute | solution.py:241
  4.3 7.5 %collective-permute-start.3 = (f32[64,512]{1,0:T(8,128)}, f32[64,512]{1,0:T(8,128)S(1)}, u32[]{:S(2)}, u32[]{:S(2)}) collective-permute-start(f32[64,512]{1,0:T(8,128)} %bitcast.57), channel_id=1, source_target_pairs={{0,64},{64,128},{128,192},{192,0},{1,65},{65,129},{129,193},{193,1... | collective-permute-start | bytes 393224 | tf_op jit(solution)/shard_map/ppermute | solution.py:241
  4.6 7.2 %collective-permute-start.1 = (f32[64,512]{1,0:T(8,128)}, f32[64,512]{1,0:T(8,128)S(1)}, u32[]{:S(2)}, u32[]{:S(2)}) collective-permute-start(f32[64,512]{1,0:T(8,128)} %bitcast.58), channel_id=1, source_target_pairs={{0,192},{64,0},{128,64},{192,128},{1,193},{65,1},{129,65},{193,129... | collective-permute-start | bytes 393224 | tf_op jit(solution)/shard_map/ppermute | solution.py:241
  12.8 5.3 %collective-permute-start.4 = (f32[4,64,512]{2,1,0:T(8,128)S(1)}, f32[4,64,512]{2,1,0:T(8,128)S(1)}, u32[]{:S(2)}, u32[]{:S(2)}) collective-permute-start(f32[4,64,512]{2,1,0:T(8,128)S(1)} %get-tuple-element.45), channel_id=1, source_target_pairs={{0,32},{32,0},{1,33},{33,1},{2,34},{34,2},{3,35},{35,3},{4,36},{36... | collective-permute-start | bytes 1572872 | tf_op jit(solution)/shard_map/ppermute | solution.py:286
  19.3 14.6 %collective-permute-start.5 = (f32[256,512]{1,0:T(8,128)S(1)}, f32[256,512]{1,0:T(8,128)S(1)}, u32[]{:S(2)}, u32[]{:S(2)}) collective-permute-start(f32[256,512]{1,0:T(8,128)S(1)} %get-tuple-element.21), channel_id=1, source_target_pairs={{0,1},{1,2},{2,3},{3,0},{4,5},{5,6},{6,7},{7,4},{8,9},{9,10},{10,1... | collective-permute-start | bytes 1572872 | tf_op jit(solution)/shard_map/ppermute | solution.py:236
  20.1 13.8 %collective-permute-start.6 = (f32[256,512]{1,0:T(8,128)S(1)}, f32[256,512]{1,0:T(8,128)S(1)}, u32[]{:S(2)}, u32[]{:S(2)}) collective-permute-start(f32[256,512]{1,0:T(8,128)S(1)} %get-tuple-element.22), channel_id=1, source_target_pairs={{0,3},{1,0},{2,1},{3,2},{4,7},{5,4},{6,5},{7,6},{8,11},{9,8},{10,9... | collective-permute-start | bytes 1572872 | tf_op jit(solution)/shard_map/ppermute | solution.py:236
  34.1 34.8 %collective-permute-start.7 = (f32[512,512]{1,0:T(8,128)S(1)}, f32[512,512]{1,0:T(8,128)}, u32[]{:S(2)}, u32[]{:S(2)}) collective-permute-start(f32[512,512]{1,0:T(8,128)S(1)} %pad_add_fusion.1), channel_id=1, source_target_pairs={{0,1},{1,2},{2,3},{3,0},{4,5},{5,6},{6,7},{7,4},{8,9},{9,10},{10,1... | collective-permute-start | bytes 3145736 | tf_op jit(solution)/shard_map/ppermute | solution.py:236
  35.8 33.1 %collective-permute-start.8 = (f32[512,512]{1,0:T(8,128)}, f32[512,512]{1,0:T(8,128)}, u32[]{:S(2)}, u32[]{:S(2)}) collective-permute-start(f32[512,512]{1,0:T(8,128)} %pad_add_fusion), channel_id=1, source_target_pairs={{0,3},{1,0},{2,1},{3,2},{4,7},{5,4},{6,5},{7,6},{8,11},{9,8},{10,9... | collective-permute-start | bytes 3145736 | tf_op jit(solution)/shard_map/ppermute | solution.py:236
  61.0 24.4 %all-to-all-start.1 = ((f32[8,64,256]{2,1,0:T(8,128)}), f32[8,64,256]{2,1,0:T(8,128)S(1)}, u32[]{:S(2)}, u32[]{:S(2)}) async-start(f32[8,64,256]{2,1,0:T(8,128)} %broadcast_in_dim.7), calls=%async_computation.1 | async-start | bytes 1048576 | tf_op jit(solution)/shard_map/all_to_all | solution.py:297
  70.8 9.7 %collective-permute-start.10 = (f32[32,512]{1,0:T(8,128)S(1)}, f32[32,512]{1,0:T(8,128)S(1)}, u32[]{:S(2)}, u32[]{:S(2)}) collective-permute-start(f32[32,512]{1,0:T(8,128)S(1)} %get-tuple-element.39), channel_id=1, source_target_pairs={{0,28},{4,0},{8,4},{12,8},{16,12},{20,16},{24,20},{28,24},{1,29},{... | collective-permute-start | bytes 196616 | tf_op jit(solution)/shard_map/ppermute | solution.py:236
  73.5 9.1 %collective-permute-start.9 = (f32[32,512]{1,0:T(8,128)S(1)}, f32[32,512]{1,0:T(8,128)S(1)}, u32[]{:S(2)}, u32[]{:S(2)}) collective-permute-start(f32[32,512]{1,0:T(8,128)S(1)} %get-tuple-element.40), channel_id=1, source_target_pairs={{0,4},{4,8},{8,12},{12,16},{16,20},{20,24},{24,28},{28,0},{1,5},{5... | collective-permute-start | bytes 196616 | tf_op jit(solution)/shard_map/ppermute | solution.py:236
  82.6 5.5 %collective-permute-start.11 = (f32[64,512]{1,0:T(8,128)S(1)}, f32[64,512]{1,0:T(8,128)S(1)}, u32[]{:S(2)}, u32[]{:S(2)}) collective-permute-start(f32[64,512]{1,0:T(8,128)S(1)} %get-tuple-element.38), channel_id=1, source_target_pairs={{0,4},{4,8},{8,12},{12,16},{16,20},{20,24},{24,28},{28,0},{1,5},{5... | collective-permute-start | bytes 393224 | tf_op jit(solution)/shard_map/ppermute | solution.py:236
  82.7 5.5 %collective-permute-start.12 = (f32[64,512]{1,0:T(8,128)S(1)}, f32[64,512]{1,0:T(8,128)S(1)}, u32[]{:S(2)}, u32[]{:S(2)}) collective-permute-start(f32[64,512]{1,0:T(8,128)S(1)} %get-tuple-element.37), channel_id=1, source_target_pairs={{0,28},{4,0},{8,4},{12,8},{16,12},{20,16},{24,20},{28,24},{1,29},{... | collective-permute-start | bytes 393224 | tf_op jit(solution)/shard_map/ppermute | solution.py:236
  85.3 11.6 %collective-permute-start = (f32[512,256]{1,0:T(8,128)S(1)}, f32[512,256]{1,0:T(8,128)S(1)}, u32[]{:S(2)}, u32[]{:S(2)}) collective-permute-start(f32[512,256]{1,0:T(8,128)S(1)} %bitcast.50), channel_id=1, source_target_pairs={{0,32},{32,0},{1,33},{33,1},{2,34},{34,2},{3,35},{35,3},{4,36},{36... | collective-permute-start | bytes 1572872 | tf_op jit(solution)/shard_map/ppermute | solution.py:286
  88.2 5.1 %collective-permute-start.13 = (f32[64,512]{1,0:T(8,128)S(1)}, f32[64,512]{1,0:T(8,128)S(1)}, u32[]{:S(2)}, u32[]{:S(2)}) collective-permute-start(f32[64,512]{1,0:T(8,128)S(1)} %get-tuple-element.36), channel_id=1, source_target_pairs={{0,4},{4,8},{8,12},{12,16},{16,20},{20,24},{24,28},{28,0},{1,5},{5... | collective-permute-start | bytes 393224 | tf_op jit(solution)/shard_map/ppermute | solution.py:236
  88.8 5.0 %collective-permute-start.14 = (f32[64,512]{1,0:T(8,128)S(1)}, f32[64,512]{1,0:T(8,128)S(1)}, u32[]{:S(2)}, u32[]{:S(2)}) collective-permute-start(f32[64,512]{1,0:T(8,128)S(1)} %get-tuple-element.35), channel_id=1, source_target_pairs={{0,28},{4,0},{8,4},{12,8},{16,12},{20,16},{24,20},{28,24},{1,29},{... | collective-permute-start | bytes 393224 | tf_op jit(solution)/shard_map/ppermute | solution.py:236
  93.9 12.0 %collective-permute-start.15 = (f32[64,512]{1,0:T(8,128)S(1)}, f32[64,512]{1,0:T(8,128)S(1)}, u32[]{:S(2)}, u32[]{:S(2)}) collective-permute-start(f32[64,512]{1,0:T(8,128)S(1)} %get-tuple-element.33), channel_id=1, source_target_pairs={{0,4},{4,8},{8,12},{12,16},{16,20},{20,24},{24,28},{28,0},{1,5},{5... | collective-permute-start | bytes 393224 | tf_op jit(solution)/shard_map/ppermute | solution.py:236
  96.9 8.9 %collective-permute-start.16 = (f32[64,512]{1,0:T(8,128)S(1)}, f32[64,512]{1,0:T(8,128)S(1)}, u32[]{:S(2)}, u32[]{:S(2)}) collective-permute-start(f32[64,512]{1,0:T(8,128)S(1)} %get-tuple-element.32), channel_id=1, source_target_pairs={{0,28},{4,0},{8,4},{12,8},{16,12},{20,16},{24,20},{28,24},{1,29},{... | collective-permute-start | bytes 393224 | tf_op jit(solution)/shard_map/ppermute | solution.py:236
  107.3 5.0 %collective-permute-start.20 = (f32[64,512]{1,0:T(8,128)S(1)}, f32[64,512]{1,0:T(8,128)S(1)}, u32[]{:S(2)}, u32[]{:S(2)}) collective-permute-start(f32[64,512]{1,0:T(8,128)S(1)} %shard_map.55), channel_id=1, source_target_pairs={{0,4},{4,8},{8,12},{12,16},{16,20},{20,24},{24,28},{28,0},{1,5},{5... | collective-permute-start | bytes 393224 | tf_op jit(solution)/shard_map/ppermute | solution.py:236
  110.5 4.7 %collective-permute-start.18 = (f32[64,512]{1,0:T(8,128)S(1)}, f32[64,512]{1,0:T(8,128)S(1)}, u32[]{:S(2)}, u32[]{:S(2)}) collective-permute-start(f32[64,512]{1,0:T(8,128)S(1)} %collective-permute-done.17), channel_id=1, source_target_pairs={{0,28},{4,0},{8,4},{12,8},{16,12},{20,16},{24,20},{28,24},{1,29},{... | collective-permute-start | bytes 393224 | tf_op jit(solution)/shard_map/ppermute | solution.py:236
  112.3 6.3 %collective-permute-start.21 = (f32[64,512]{1,0:T(8,128)S(1)}, f32[64,512]{1,0:T(8,128)S(1)}, u32[]{:S(2)}, u32[]{:S(2)}) collective-permute-start(f32[64,512]{1,0:T(8,128)S(1)} %collective-permute-done.20), channel_id=1, source_target_pairs={{0,4},{4,8},{8,12},{12,16},{16,20},{20,24},{24,28},{28,0},{1,5},{5... | collective-permute-start | bytes 393224 | tf_op jit(solution)/shard_map/ppermute | solution.py:236
  115.2 8.5 %collective-permute-start.19 = (f32[64,512]{1,0:T(8,128)S(1)}, f32[64,512]{1,0:T(8,128)S(1)}, u32[]{:S(2)}, u32[]{:S(2)}) collective-permute-start(f32[64,512]{1,0:T(8,128)S(1)} %collective-permute-done.18), channel_id=1, source_target_pairs={{0,28},{4,0},{8,4},{12,8},{16,12},{20,16},{24,20},{28,24},{1,29},{... | collective-permute-start | bytes 393224 | tf_op jit(solution)/shard_map/ppermute | solution.py:236
  118.6 5.0 %collective-permute-start.22 = (f32[64,512]{1,0:T(8,128)S(1)}, f32[64,512]{1,0:T(8,128)S(1)}, u32[]{:S(2)}, u32[]{:S(2)}) collective-permute-start(f32[64,512]{1,0:T(8,128)S(1)} %collective-permute-done.21), channel_id=1, source_target_pairs={{0,4},{4,8},{8,12},{12,16},{16,20},{20,24},{24,28},{28,0},{1,5},{5... | collective-permute-start | bytes 393224 | tf_op jit(solution)/shard_map/ppermute | solution.py:236
  123.7 4.6 %collective-permute-start.24 = (f32[32,512]{1,0:T(8,128)S(1)}, f32[32,512]{1,0:T(8,128)S(1)}, u32[]{:S(2)}, u32[]{:S(2)}) collective-permute-start(f32[32,512]{1,0:T(8,128)S(1)} %slice.90), channel_id=1, source_target_pairs={{0,28},{4,0},{8,4},{12,8},{16,12},{20,16},{24,20},{28,24},{1,29},{... | collective-permute-start | bytes 196616 | tf_op jit(solution)/shard_map/ppermute | solution.py:236
  128.4 17.4 %collective-permute-start.25 = (f32[512,512]{1,0:T(8,128)S(1)}, f32[512,512]{1,0:T(8,128)S(1)}, u32[]{:S(2)}, u32[]{:S(2)}) collective-permute-start(f32[512,512]{1,0:T(8,128)S(1)} %constant_dynamic-update-slice_fusion.own.refs_2_), channel_id=1, source_target_pairs={{0,1},{1,2},{2,3},{3,0},{4,5},{5,6},{6,7},{7,4},{8,9},{9,10},{10,1... | collective-permute-start | bytes 3145736 | tf_op jit(solution)/shard_map/ppermute | solution.py:236
  130.4 15.5 %collective-permute-start.27 = (f32[512,512]{1,0:T(8,128)S(1)}, f32[512,512]{1,0:T(8,128)S(1)}, u32[]{:S(2)}, u32[]{:S(2)}) collective-permute-start(f32[512,512]{1,0:T(8,128)S(1)} %constant_dynamic-update-slice_fusion.own.refs_2_), channel_id=1, source_target_pairs={{0,3},{1,0},{2,1},{3,2},{4,7},{5,4},{6,5},{7,6},{8,11},{9,8},{10,9... | collective-permute-start | bytes 3145736 | tf_op jit(solution)/shard_map/ppermute | solution.py:236
  145.8 15.0 %collective-permute-start.26 = (f32[256,512]{1,0:T(8,128)S(1)}, f32[256,512]{1,0:T(8,128)S(1)}, u32[]{:S(2)}, u32[]{:S(2)}) collective-permute-start(f32[256,512]{1,0:T(8,128)S(1)} %slice.91), channel_id=1, source_target_pairs={{0,1},{1,2},{2,3},{3,0},{4,5},{5,6},{6,7},{7,4},{8,9},{9,10},{10,1... | collective-permute-start | bytes 1572872 | tf_op jit(solution)/shard_map/ppermute | solution.py:236
  145.9 14.9 %collective-permute-start.28 = (f32[256,512]{1,0:T(8,128)S(1)}, f32[256,512]{1,0:T(8,128)S(1)}, u32[]{:S(2)}, u32[]{:S(2)}) collective-permute-start(f32[256,512]{1,0:T(8,128)S(1)} %slice.92), channel_id=1, source_target_pairs={{0,3},{1,0},{2,1},{3,2},{4,7},{5,4},{6,5},{7,6},{8,11},{9,8},{10,9... | collective-permute-start | bytes 1572872 | tf_op jit(solution)/shard_map/ppermute | solution.py:236
  162.1 12.5 %collective-permute-start.29 = (f32[4,64,512]{2,1,0:T(8,128)S(1)}, f32[4,64,512]{2,1,0:T(8,128)S(1)}, u32[]{:S(2)}, u32[]{:S(2)}) collective-permute-start(f32[4,64,512]{2,1,0:T(8,128)S(1)} %slice_bitcast_fusion), channel_id=1, source_target_pairs={{0,32},{32,0},{1,33},{33,1},{2,34},{34,2},{3,35},{35,3},{4,36},{36... | collective-permute-start | bytes 1572872 | tf_op jit(solution)/shard_map/ppermute | solution.py:286
  174.8 8.1 %collective-permute-start.30 = (f32[64,512]{1,0:T(8,128)S(1)}, f32[64,512]{1,0:T(8,128)S(1)}, u32[]{:S(2)}, u32[]{:S(2)}) collective-permute-start(f32[64,512]{1,0:T(8,128)S(1)} %get-tuple-element.41), channel_id=1, source_target_pairs={{0,64},{64,128},{128,192},{192,0},{1,65},{65,129},{129,193},{193,1... | collective-permute-start | bytes 393224 | tf_op jit(solution)/shard_map/ppermute | solution.py:241
  176.6 6.2 %collective-permute-start.31 = (f32[64,512]{1,0:T(8,128)S(1)}, f32[64,512]{1,0:T(8,128)S(1)}, u32[]{:S(2)}, u32[]{:S(2)}) collective-permute-start(f32[64,512]{1,0:T(8,128)S(1)} %get-tuple-element.43), channel_id=1, source_target_pairs={{0,192},{64,0},{128,64},{192,128},{1,193},{65,1},{129,65},{193,129... | collective-permute-start | bytes 393224 | tf_op jit(solution)/shard_map/ppermute | solution.py:241
  177.8 7.1 %collective-permute-start.32 = (f32[64,512]{1,0:T(8,128)S(1)}, f32[64,512]{1,0:T(8,128)S(1)}, u32[]{:S(2)}, u32[]{:S(2)}) collective-permute-start(f32[64,512]{1,0:T(8,128)S(1)} %get-tuple-element.42), channel_id=1, source_target_pairs={{0,128},{64,192},{128,0},{192,64},{1,129},{65,193},{129,1},{193,65... | collective-permute-start | bytes 393224 | tf_op jit(solution)/shard_map/ppermute | solution.py:241
  (6 other events, 100.2 us)
where the time goes:
time: 187 us; the launch traced here: 186 us
  starting transfers between devices  66 us (35%)
  waiting for transfers between devices  62.9 us (34%)
  Pallas kernels  23.7 us (13%)
  blocking collectives  22.1 us (12%)
  other arithmetic  5.42 us (3%)
  local copies, waits for them, and re-layouts  3.45 us (2%)
    ppermute x12, waiting for transfers between devices, ring(): lax.ppermute(v, axis, right)  41.6 us
    ppermute x12, starting transfers between devices, ring(): lax.ppermute(v, axis, left)  24.4 us
    all_to_all x1, blocking collectives, steps(): part = lax.all_to_all(copies, axis, split_axis=0, concat_axis=0, tiled=True)  22.1 us
    ppermute x3, starting transfers between devices, steps(): swap = lambda v: lax.ppermute(v, 'core', [(0, 1), (1, 0)])  15.1 us
    ppermute x12, waiting for transfers between devices, ring(): lax.ppermute(v, axis, left)  12.9 us
    ppermute x6, starting transfers between devices, shifted(): return lax.ppermute(value, axis, [(i, (i + hops) % n) for i in range(n)])  10.5 us
    ppermute x12, starting transfers between devices, ring(): lax.ppermute(v, axis, right)  8.11 us
    all_to_all x1, starting transfers between devices, steps(): part = lax.all_to_all(copies, axis, split_axis=0, concat_axis=0, tiled=True)  7.87 us
  transfers between devices with their start and end apart: 34, of which 15 were waited for; matrix products, arithmetic and copies ran while one was open for 2% of the time, Pallas kernels for 12%

commit v1 on v0

--- a/solution.py
+++ b/solution.py
@@ -16,6 +16,7 @@
 BLK = 512
 ROWS = 2048
 PIECE = ROWS // NCOL
+HALF = PIECE // 2
 CHUNK = NZ * PIECE
 WIDTH = 4
 TILE = 128
@@ -32,7 +33,7 @@
 NN = (((1,), (0,)), ((), ()))
 
 
-def call(kernel, out, n_in, flops=0, scratch=(), smem=True, mib=8):
+def call(kernel, out, n_in, flops=0, scratch=(), smem=True, mib=8, aliases=None):
     many = isinstance(out, (list, tuple))
     return pl.pallas_call(
         kernel,
@@ -40,6 +41,7 @@
         in_specs=([SMEM] if smem else []) + [VMEM] * n_in,
         out_specs=[VMEM] * len(out) if many else VMEM,
         scratch_shapes=list(scratch),
+        input_output_aliases=aliases or {},
         compiler_params=pltpu.CompilerParams(vmem_limit_bytes=mib << 20),
         cost_estimate=pl.CostEstimate(flops=flops, bytes_accessed=1 << 20, transcendentals=0),
     )
@@ -84,12 +86,17 @@
             out[place, :] = lower + jnp.where(row == col, 1.0, 0.0)
 
     for dy, offset in OFFSET.items():
-        owner_y = lax.rem(y + dy, NY)
-
-        @pl.loop(0, NZ)
-        def _(dz):
-            owner_z = lax.rem(z + dz, NZ)
-            piece(owner_y * CHUNK + owner_z * PIECE, offset + dz * PIECE, PIECE)
+        for group in range(4):
+
+            @pl.loop(0, NZ // 2)
+            def _(k):
+                piece(own_rows(z, y, dy, group, k), offset + group * (CHUNK // 4) + k * HALF, HALF)
+
+
+def own_rows(z, y, dy, group, k):
+    parity = z & 1
+    first, half = ((1, parity), (7, 1 - parity), (0, 1 - parity), (0, parity))[group]
+    return ((y + dy) & (NY - 1)) * CHUNK + ((z + first + 2 * k) & (NZ - 1)) * PIECE + half * HALF
 
 
 def merge(a, b):
@@ -205,35 +212,46 @@
     out[...] = -dot_full(a0[...] + a1[...] + a2[...], x11[...])
 
 
-def columns_kernel(idx, far_low, far_up, up, down, own, out, held):
+def take_columns(idx, dys, sources, held):
     x, core, z, y = idx[0], idx[1], idx[2], idx[3]
     column = z * NY + y
     tile = lax.rem((column >> 3) - x + NX, NX)
     inside = ((((column >> 2) & 1) + core) & 1) * 64 + (column & 3) * 16
     lanes = pl.ds(pl.multiple_of(tile * 128, 128), 128)
     turn = lax.rem(128 - inside, 128)
-    half = CHUNK // 2
-    for dy, source, first, size in (
-        (2, far_low, 0, half), (2, far_up, half, half), (1, up, 0, CHUNK), (3, down, 0, CHUNK), (0, own, 0, CHUNK)
-    ):
-        owner_y = lax.rem(y + dy, NY)
-
-        @pl.loop(0, size // PIECE)
-        def _(k):
-            owner_z = lax.rem(z + k + first // PIECE, NZ)
-            start = pl.multiple_of(k * PIECE, PIECE)
-            target = pl.multiple_of(owner_y * CHUNK + owner_z * PIECE, PIECE)
-            value = source[pl.ds(start, PIECE), lanes]
-            held[pl.ds(target, PIECE), :] = pltpu.roll(value, turn, 1)
-
-    out[...] = held[...].T[:16, :]
-
-
-def ring(axis):
+    for dy, parts in zip(dys, sources):
+        base = ((y + dy) & (NY - 1)) * CHUNK
+        for group in range(4):
+            source = parts[group * len(parts) // 4]
+            first = group % (4 // len(parts)) * (CHUNK // 4)
+
+            @pl.loop(0, NZ // 2)
+            def _(k):
+                start = pl.multiple_of(first + k * HALF, HALF)
+                target = pl.multiple_of(own_rows(z, y, dy, group, k) - base, HALF)
+                value = source[pl.ds(start, HALF), lanes]
+                held[pl.ds(target, HALF), :] = pltpu.roll(value, turn, 1)
+
+        yield pl.ds(pl.multiple_of(base, CHUNK), CHUNK), held[...].T[:16, :]
+
+
+def near_columns_kernel(idx, up, down, own, out, held):
+    out[...] = jnp.zeros_like(out)
+    for place, value in take_columns(idx, ORDER[1:], ((up,), (down,), (own,)), held):
+        out[:, place] = value
+
+
+def far_columns_kernel(idx, near, low, up, out, held):
+    out[...] = near[...]
+    for place, value in take_columns(idx, ORDER[:1], ((low, up),), held):
+        out[:, place] = value
+
+
+def ring(axis, stride=1):
     n = lax.axis_size(axis)
-    right = [(i, (i + 1) % n) for i in range(n)]
-    left = [(i, (i - 1) % n) for i in range(n)]
-    return n, lambda v: lax.ppermute(v, axis, right), lambda v: lax.ppermute(v, axis, left)
+    right = [(i, (i + stride) % n) for i in range(n)]
+    left = [(i, (i - stride) % n) for i in range(n)]
+    return lambda v: lax.ppermute(v, axis, right), lambda v: lax.ppermute(v, axis, left)
 
 
 def shifted(value, axis, hops):
@@ -241,36 +259,27 @@
     return lax.ppermute(value, axis, [(i, (i + hops) % n) for i in range(n)])
 
 
-def sum_to_owner(chunks, far, axis):
-    n, right, left = ring(axis)
-    half = far[0].shape[0]
+def sum_of_four(chunks, far, axis, stride=1):
+    right, left = ring(axis, stride)
     a, b = right(far[0]), left(far[1])
-    for hop in range(n // 2 - 1, 0, -1):
-        a, b = lax.optimization_barrier((a, b))
-        if hop == n // 2 - 1:
-            a = jnp.pad(a, ((0, half), (0, 0)))
-            b = jnp.pad(b, ((half, 0), (0, 0)))
-        up, down = chunks[hop] + a, chunks[n - hop] + b
-        a, b = right(up), left(down)
-    return chunks[0], a, b
-
-
-def gather(own, axis):
-    n, right, left = ring(axis)
+    rows = jax.ShapeDtypeStruct(chunks[1].shape, jnp.float32)
+    up, down = call(middle_kernel, [rows] * 2, 4, 10**6, smem=False, aliases={0: 0, 1: 1})(
+        chunks[1], chunks[3], a, b
+    )
+    return chunks[0], right(up), left(down)
+
+
+def middle_kernel(up, down, a, b, up_out, down_out):
+    half = a.shape[0]
+    up_out[:half, :] = up[:half, :] + a[...]
+    down_out[half:, :] = down[half:, :] + b[...]
+
+
+def gather_of_four(own, axis, stride=1):
+    right, left = ring(axis, stride)
     half = own.shape[0] // 2
-    chunks = {0: own}
-    a = b = own
-    for hop in range(1, n // 2):
-        a, b = right(a), left(b)
-        chunks[n - hop], chunks[hop] = a, b
-    return chunks, right(a[:half]), left(b[half:])
-
-
-def joined(chunks, n, lower, upper):
-    parts = []
-    for hop in range(n):
-        parts += [lower, upper] if hop == n // 2 else [chunks[hop]]
-    return jnp.concatenate(parts, axis=0)
+    a, b = right(own), left(own)
+    return {0: own, 1: b, 3: a}, right(a[:half]), left(b[half:])
 
 
 def dot_high(a, b, dims):
@@ -326,31 +335,37 @@
     later = product(CHUNK, [shape((CHUNK, BLK), f32)] * 3)
     partial = dict(zip(ORDER[1:], later))
 
-    part = sum(sum_to_owner(partial, far, "y"))
-    parts = {d: part[d * PIECE : (d + 1) * PIECE] for d in range(NZ)}
-    cut = NZ // 2 * PIECE + PIECE // 2
-    far = (part[cut - PIECE // 2 : cut], part[cut : cut + PIECE // 2])
-    parts = sum_to_owner(parts, far, "z")
+    part = sum(sum_of_four(partial, far, "y"))
+    right, left = ring("z")
+    quarter = CHUNK // 4
+    a, b = right(part[:quarter]), left(part[quarter : 2 * quarter])
+    a, b = lax.optimization_barrier((a, b))
+    a = part[2 * quarter : 3 * quarter] + a
+    b = part[3 * quarter :] + b
+    spots = [slice(k * HALF, (k + 1) * HALF) for k in range(4)]
+    pieces = {k: jnp.concatenate([a[spots[k]], b[spots[k]]], axis=0) for k in (0, 1, 3)}
+    parts = sum_of_four(pieces, (a[spots[2]], b[spots[2]]), "z", 2)
     own = call(scale_kernel, shape((PIECE, BLK), f32), 4, 12 * PIECE * BLK * BLK, smem=False)(x11, *parts)
-    own = joined_gather(own, "z")
-    chunks, far_low, far_up = gather(own, "y")
+    near, low, up = gather_of_four(own, "z", 2)
+    a = jnp.concatenate([near[0][:HALF], near[1][:HALF], low, near[3][:HALF]], axis=0)
+    b = jnp.concatenate([near[0][HALF:], near[1][HALF:], up, near[3][HALF:]], axis=0)
+    own = jnp.concatenate([left(a), right(b), a, b], axis=0)
+    chunks, far_low, far_up = gather_of_four(own, "y")
     total = call(
         near_kernel, shape((BLK, BLK), f32), 4, 6 * (ROWS - CHUNK) * BLK * BLK, smem=False, mib=14
     )(w, *[chunks[dy] for dy in ORDER[1:]])
     update = total + dot_high(jnp.concatenate([far_low, far_up], axis=0), w[:CHUNK], TN)
-    columns = call(
-        columns_kernel, shape((16, ROWS), f32), 5, 10**7, scratch=[pltpu.VMEM((ROWS, 128), f32)]
-    )(idx, far_low, far_up, chunks[1], chunks[3], own)
+    held = [pltpu.VMEM((CHUNK, 128), f32)]
+    strip = shape((16, ROWS), f32)
+    columns = call(near_columns_kernel, strip, 3, 10**7, scratch=held)(
+        idx, *[chunks[dy] for dy in ORDER[1:]]
+    )
+    columns = call(far_columns_kernel, strip, 3, 10**7, scratch=held)(idx, columns, far_low, far_up)
 
     blocks = update.reshape(NX, NC, 64, BLK)
     rows = blocks[:, 0] + swap(blocks[:, 1])
     product = rows[0] + shifted(rows[1], "x", 1) + shifted(rows[3], "x", -1) + shifted(rows[2], "x", 2)
     return columns.T, product.T
-
-
-def joined_gather(own, axis):
-    chunks, lower, upper = gather(own, axis)
-    return joined(chunks, lax.axis_size(axis), lower, upper)
 
 
 def solution(mesh):

time: 187 us -> 192 us (1.027)
  blocking collectives: 22.1 us -> 45.1 us
  starting transfers between devices: 66 us -> 54.3 us
  waiting for transfers between devices: 62.9 us -> 55.1 us
  Pallas kernels: 23.7 us -> 27.4 us
  other arithmetic: 5.42 us -> 2.68 us
  local copies, waits for them, and re-layouts: 3.45 us -> 5.58 us
    all_to_all x1 -> x2, blocking collectives: 22.1 us -> 45.1 us  [steps(): part = lax.all_to_all(copies, axis, split_axis=0, concat_axis=0, tiled=True)]
    all_to_all x1 -> x0, starting transfers between devices: 7.87 us -> none  [steps(): part = lax.all_to_all(copies, axis, split_axis=0, concat_axis=0, tiled=True)]
    ppermute x12 -> x10, waiting for transfers between devices: 12.9 us -> 7.76 us  [ring(): lax.ppermute(v, axis, left)]
    ppermute x12 -> x10, starting transfers between devices: 24.4 us -> 20.5 us  [ring(): lax.ppermute(v, axis, left)]
    pallas_call x1 -> x4, Pallas kernels: 3.92 us -> 6.93 us  [the longest x1 4.27 us: steps(): call(near_columns_kernel, strip, 3, 10 ** 7, scratch=held)]
    unnamed x16 -> x19, local copies, waits for them, and re-layouts: 2.28 us -> 5.22 us
    add x6 -> x2, other arithmetic: 3.24 us -> 0.43 us  [the longest x1 0.35 us: steps(): part = sum(sum_of_four(partial, far, 'y'))]
    ppermute x6, waiting for transfers between devices: 6.89 us -> 4.8 us  [shifted(): return lax.ppermute(value, axis, [(i, (i + hops) % n) for i in range(n)])]
  transfers between devices with their start and end apart: 34 -> 29, of which waited for: 15 -> 12; matrix products, arithmetic and copies ran while one was open for 2% -> 0% of each run, Pallas kernels for 12% -> 13%
where the time goes in v1:
time: 192 us
  waiting for transfers between devices  55.1 us (29%)
  starting transfers between devices  54.3 us (28%)
  blocking collectives  45.1 us (23%)
  Pallas kernels  27.4 us (14%)
  local copies, waits for them, and re-layouts  5.58 us (3%)
  other arithmetic  2.68 us (1%)
    all_to_all x2, blocking collectives, steps(): part = lax.all_to_all(copies, axis, split_axis=0, concat_axis=0, tiled=True)  45.1 us
    ppermute x10, waiting for transfers between devices, ring(): lax.ppermute(v, axis, right)  41 us
    ppermute x10, starting transfers between devices, ring(): lax.ppermute(v, axis, left)  20.5 us
    ppermute x3, starting transfers between devices, steps(): swap = lambda v: lax.ppermute(v, 'core', [(0, 1), (1, 0)])  15.6 us
    ppermute x6, starting transfers between devices, shifted(): return lax.ppermute(value, axis, [(i, (i + hops) % n) for i in range(n)])  10.6 us
    ppermute x10, waiting for transfers between devices, ring(): lax.ppermute(v, axis, left)  7.76 us
    ppermute x10, starting transfers between devices, ring(): lax.ppermute(v, axis, right)  7.59 us
    pallas_call x1, Pallas kernels, steps(): call(inverse_kernel, square, 2, 10 ** 9, scratch=[pltpu.VMEM((BLK, BLK),...  5.61 us
  transfers between devices with their start and end apart: 29, of which 12 were waited for; matrix products, arithmetic and copies ran while one was open for 0% of the time, Pallas kernels for 13%

profile of v1, /device:TPU:1, one launch (start us, length us, event | category | flops | bytes accessed | tf_op | source)
XLA Modules:
  0.0 192.2 jit_solution(12299690918926052880)
XLA Ops:
  0.6 3.6 %collective-permute-start.2 = (f32[64,512]{1,0:T(8,128)}, f32[64,512]{1,0:T(8,128)S(1)}, u32[]{:S(2)}, u32[]{:S(2)}) collective-permute-start(f32[64,512]{1,0:T(8,128)} %bitcast.56), channel_id=1, source_target_pairs={{0,128},{64,192},{128,0},{192,64},{1,129},{65,193},{129,1},{193,65... | collective-permute-start | bytes 393224 | tf_op jit(solution)/shard_map/ppermute | solution.py:259
  4.6 2.4 %collective-permute-start.1 = (f32[64,512]{1,0:T(8,128)}, f32[64,512]{1,0:T(8,128)S(1)}, u32[]{:S(2)}, u32[]{:S(2)}) collective-permute-start(f32[64,512]{1,0:T(8,128)} %bitcast.58), channel_id=1, source_target_pairs={{0,192},{64,0},{128,64},{192,128},{1,193},{65,1},{129,65},{193,129... | collective-permute-start | bytes 393224 | tf_op jit(solution)/shard_map/ppermute | solution.py:259
  7.0 4.8 %collective-permute-done.3 = f32[64,512]{1,0:T(8,128)S(1)} collective-permute-done((f32[64,512]{1,0:T(8,128)}, f32[64,512]{1,0:T(8,128)S(1)}, u32[]{:S(2)}, u32[]{:S(2)}) %collective-permute-start.3) | collective-permute-done | bytes 131104 | tf_op jit(solution)/shard_map/ppermute | solution.py:259
  14.2 2.2 %copy-done.4 = f32[2048,512]{1,0:T(8,128)S(1)} copy-done((f32[2048,512]{1,0:T(8,128)S(1)}, f32[2048,512]{1,0:T(8,128)}, u32[]{:S(2)}) %copy-start.4) | copy-done | bytes 4194328
  16.4 2.3 %shard_map.52.w = f32[2048,512]{1,0:T(8,128)S(1)} custom-call(s32[4]{0:T(128)S(1)} %pad_add_fusion.idx, f32[2048,512]{1,0:T(8,128)S(1)} %copy-done.4), custom_call_target="tpu_custom_call" | custom-call | flops 100000000 | bytes 1048576 | tf_op jit(solution)/shard_map/pallas_call | solution.py:320
  21.4 2.0 %collective-permute-start.6 = (f32[256,512]{1,0:T(8,128)S(1)}, f32[256,512]{1,0:T(8,128)S(1)}, u32[]{:S(2)}, u32[]{:S(2)}) collective-permute-start(f32[256,512]{1,0:T(8,128)S(1)} %get-tuple-element.21), channel_id=1, source_target_pairs={{0,3},{1,0},{2,1},{3,2},{4,7},{5,4},{6,5},{7,6},{8,11},{9,8},{10,9... | collective-permute-start | bytes 1572872 | tf_op jit(solution)/shard_map/ppermute | solution.py:254
  23.4 2.2 %copy-done.2 = f32[2048,512]{1,0:T(8,128)S(1)} copy-done((f32[2048,512]{1,0:T(8,128)S(1)}, f32[2048,512]{1,0:T(8,128)}, u32[]{:S(2)}) %copy-start.2) | copy-done | bytes 4194328
  25.6 3.8 %shard_map.53 = (f32[512,512]{1,0:T(8,128)S(1)}, f32[512,512]{1,0:T(8,128)S(1)}, f32[512,512]{1,0:T(8,128)S(1)}) custom-call(f32[512,512]{1,0:T(8,128)S(1)} %bitcast.49, f32[2048,512]{1,0:T(8,128)S(1)} %copy-done.2), custom_call_target="tpu_custom_call" | custom-call | flops 2415919104 | bytes 1048576 | tf_op jit(solution)/shard_map/pallas_call | solution.py:324
  29.4 5.9 %collective-permute-done.5.a = f32[256,512]{1,0:T(8,128)S(1)} collective-permute-done((f32[256,512]{1,0:T(8,128)S(1)}, f32[256,512]{1,0:T(8,128)S(1)}, u32[]{:S(2)}, u32[]{:S(2)}) %collective-permute-start.5) | collective-permute-done | bytes 524320 | tf_op jit(solution)/shard_map/ppermute | solution.py:254
  36.0 2.2 %collective-permute-start.8 = (f32[512,512]{1,0:T(8,128)S(1)}, f32[512,512]{1,0:T(8,128)S(1)}, u32[]{:S(2)}, u32[]{:S(2)}) collective-permute-start(f32[512,512]{1,0:T(8,128)S(1)} %get-tuple-element.23), channel_id=1, source_target_pairs={{0,3},{1,0},{2,1},{3,2},{4,7},{5,4},{6,5},{7,6},{8,11},{9,8},{10,9... | collective-permute-start | bytes 3145736 | tf_op jit(solution)/shard_map/ppermute | solution.py:254
  38.2 23.2 %all_to_all.10 = f32[4,16,256]{2,1,0:T(8,128)S(1)} all-to-all(f32[4,16,256]{2,1,0:T(8,128)S(1)} %broadcast_in_dim.6), channel_id=1, replica_groups=mesh['x'=4,'core'=2,'z'=8,'y'=4] {'y'}, dimensions={0} | all-to-all | bytes 131072 | tf_op jit(solution)/shard_map/all_to_all | solution.py:306
  61.5 21.8 %all_to_all.11 = f32[8,64,256]{2,1,0:T(8,128)S(1)} all-to-all(f32[8,64,256]{2,1,0:T(8,128)S(1)} %broadcast_in_dim.7), channel_id=1, replica_groups=mesh['x'=4,'core'=2,'z'=8,'y'=4] {'z'}, dimensions={0} | all-to-all | bytes 1048576 | tf_op jit(solution)/shard_map/all_to_all | solution.py:306
  83.3 4.0 %collective-permute-start = (f32[512,256]{1,0:T(8,128)S(1)}, f32[512,256]{1,0:T(8,128)S(1)}, u32[]{:S(2)}, u32[]{:S(2)}) collective-permute-start(f32[512,256]{1,0:T(8,128)S(1)} %bitcast.50), channel_id=1, source_target_pairs={{0,32},{32,0},{1,33},{33,1},{2,34},{34,2},{3,35},{35,3},{4,36},{36... | collective-permute-start | bytes 1572872 | tf_op jit(solution)/shard_map/ppermute | solution.py:295
  89.3 3.3 %shard_map.50 = (f32[512,512]{1,0:T(8,128)S(1)}, f32[512,512]{1,0:T(8,128)S(1)}) custom-call(s32[4]{0:T(128)S(1)} %pad_add_fusion.idx, f32[512,256]{1,0:T(8,128)S(1)} %bitcast.51, f32[512,256]{1,0:T(8,128)S(1)} %collective-permute-done.other), custom_call_target="tpu_custom_call" | custom-call | flops 1000000000 | bytes 1048576 | tf_op jit(solution)/shard_map/pallas_call | solution.py:311
  92.6 3.1 %collective-permute-done.10 = f32[128,512]{1,0:T(8,128)S(1)} collective-permute-done((f32[128,512]{1,0:T(8,128)S(1)}, f32[128,512]{1,0:T(8,128)S(1)}, u32[]{:S(2)}, u32[]{:S(2)}) %collective-permute-start.10) | collective-permute-done | bytes 262176 | tf_op jit(solution)/shard_map/ppermute | solution.py:254
  97.4 3.6 %collective-permute-start.12 = (f32[32,512]{1,0:T(8,128)S(1)}, f32[32,512]{1,0:T(8,128)S(1)}, u32[]{:S(2)}, u32[]{:S(2)}) collective-permute-start(f32[32,512]{1,0:T(8,128)S(1)} %get-tuple-element.37), channel_id=1, source_target_pairs={{0,24},{4,28},{8,0},{12,4},{16,8},{20,12},{24,16},{28,20},{1,25},{... | collective-permute-start | bytes 196616 | tf_op jit(solution)/shard_map/ppermute | solution.py:254
  101.0 1.9 collective-permute-done.11.a
  102.9 2.1 %collective-permute-start.13 = (f32[64,512]{1,0:T(8,128)S(1)}, f32[64,512]{1,0:T(8,128)S(1)}, u32[]{:S(2)}, u32[]{:S(2)}) collective-permute-start(f32[64,512]{1,0:T(8,128)S(1)} %get-tuple-element.26), channel_id=1, source_target_pairs={{0,8},{4,12},{8,16},{12,20},{16,24},{20,28},{24,0},{28,4},{1,9},{5... | collective-permute-start | bytes 393224 | tf_op jit(solution)/shard_map/ppermute | solution.py:254
  106.7 5.6 %shard_map.51.x11 = f32[512,512]{1,0:T(8,128)S(1)} custom-call(s32[4]{0:T(128)S(1)} %pad_add_fusion.idx, f32[512,512]{1,0:T(8,128)S(1)} %get-tuple-element.15.u, f32[512,512]{1,0:T(8,128)S(1)} %get-tuple-element.16.diagonal), custom_call_target="tpu_custom_call" | custom-call | flops 1000000000 | bytes 1048576 | tf_op jit(solution)/shard_map/pallas_call | solution.py:312
  113.0 2.4 %collective-permute-start.15 = (f32[64,512]{1,0:T(8,128)S(1)}, f32[64,512]{1,0:T(8,128)S(1)}, u32[]{:S(2)}, u32[]{:S(2)}) collective-permute-start(f32[64,512]{1,0:T(8,128)S(1)} %shard_map.57), channel_id=1, source_target_pairs={{0,24},{4,28},{8,0},{12,4},{16,8},{20,12},{24,16},{28,20},{1,25},{... | collective-permute-start | bytes 393224 | tf_op jit(solution)/shard_map/ppermute | solution.py:254
  115.5 5.8 %collective-permute-done.16 = f32[64,512]{1,0:T(8,128)S(1)} collective-permute-done((f32[64,512]{1,0:T(8,128)S(1)}, f32[64,512]{1,0:T(8,128)S(1)}, u32[]{:S(2)}, u32[]{:S(2)}) %collective-permute-start.16) | collective-permute-done | bytes 131104 | tf_op jit(solution)/shard_map/ppermute | solution.py:254
  121.5 3.6 %collective-permute-start.19 = (f32[32,512]{1,0:T(8,128)S(1)}, f32[32,512]{1,0:T(8,128)S(1)}, u32[]{:S(2)}, u32[]{:S(2)}) collective-permute-start(f32[32,512]{1,0:T(8,128)S(1)} %get-tuple-element.47), channel_id=1, source_target_pairs={{0,24},{4,28},{8,0},{12,4},{16,8},{20,12},{24,16},{28,20},{1,25},{... | collective-permute-start | bytes 196616 | tf_op jit(solution)/shard_map/ppermute | solution.py:254
  125.1 2.1 %collective-permute-done.17 = f32[32,512]{1,0:T(8,128)S(1)} collective-permute-done((f32[32,512]{1,0:T(8,128)S(1)}, f32[32,512]{1,0:T(8,128)S(1)}, u32[]{:S(2)}, u32[]{:S(2)}) %collective-permute-start.17) | collective-permute-done | bytes 65568 | tf_op jit(solution)/shard_map/ppermute | solution.py:254
  129.0 4.6 %collective-permute-done.18 = f32[128,512]{1,0:T(8,128)S(1)} collective-permute-done((f32[128,512]{1,0:T(8,128)S(1)}, f32[128,512]{1,0:T(8,128)S(1)}, u32[]{:S(2)}, u32[]{:S(2)}) %collective-permute-start.18) | collective-permute-done | bytes 262176 | tf_op jit(solution)/shard_map/ppermute | solution.py:254
  136.1 2.3 %collective-permute-start.21 = (f32[512,512]{1,0:T(8,128)S(1)}, f32[512,512]{1,0:T(8,128)S(1)}, u32[]{:S(2)}, u32[]{:S(2)}) collective-permute-start(f32[512,512]{1,0:T(8,128)S(1)} %constant_dynamic-update-slice_fusion.own.refs_2_), channel_id=1, source_target_pairs={{0,3},{1,0},{2,1},{3,2},{4,7},{5,4},{6,5},{7,6},{8,11},{9,8},{10,9... | collective-permute-start | bytes 3145736 | tf_op jit(solution)/shard_map/ppermute | solution.py:254
  138.3 15.1 %collective-permute-done.22.down.refs_1_ = f32[512,512]{1,0:T(8,128)S(1)} collective-permute-done((f32[512,512]{1,0:T(8,128)S(1)}, f32[512,512]{1,0:T(8,128)S(1)}, u32[]{:S(2)}, u32[]{:S(2)}) %collective-permute-start.22) | collective-permute-done | bytes 1048608 | tf_op jit(solution)/shard_map/ppermute | solution.py:254
  153.6 2.7 %collective-permute-start.24 = (f32[256,512]{1,0:T(8,128)S(1)}, f32[256,512]{1,0:T(8,128)S(1)}, u32[]{:S(2)}, u32[]{:S(2)}) collective-permute-start(f32[256,512]{1,0:T(8,128)S(1)} %slice.129), channel_id=1, source_target_pairs={{0,3},{1,0},{2,1},{3,2},{4,7},{5,4},{6,5},{7,6},{8,11},{9,8},{10,9... | collective-permute-start | bytes 1572872 | tf_op jit(solution)/shard_map/ppermute | solution.py:254
  156.3 3.8 %shard_map.60 = f32[512,512]{1,0:T(8,128)S(1)} custom-call(f32[2048,512]{1,0:T(8,128)S(1)} %copy-done.3, f32[512,512]{1,0:T(8,128)S(1)} %collective-permute-done.21.up.refs_0_, f32[512,512]{1,0:T(8,128)S(1)} %collective-permute-done.22.down.refs_1_, f32[512,512]{1,0:T(8,128)S(1)} %constant_dynamic-update-slice_fusion.own.refs_2_), custom_call_target="tpu_custom_call" | custom-call | flops 2415919104 | bytes 1048576 | tf_op jit(solution)/shard_map/pallas_call | solution.py:354
  160.1 7.3 %collective-permute-done.23.low = f32[256,512]{1,0:T(8,128)S(1)} collective-permute-done((f32[256,512]{1,0:T(8,128)S(1)}, f32[256,512]{1,0:T(8,128)S(1)}, u32[]{:S(2)}, u32[]{:S(2)}) %collective-permute-start.23) | collective-permute-done | bytes 524320 | tf_op jit(solution)/shard_map/ppermute | solution.py:254
  168.7 10.2 %collective-permute-start.25 = (f32[4,64,512]{2,1,0:T(8,128)S(1)}, f32[4,64,512]{2,1,0:T(8,128)S(1)}, u32[]{:S(2)}, u32[]{:S(2)}) collective-permute-start(f32[4,64,512]{2,1,0:T(8,128)S(1)} %slice_bitcast_fusion), channel_id=1, source_target_pairs={{0,32},{32,0},{1,33},{33,1},{2,34},{34,2},{3,35},{35,3},{4,36},{36... | collective-permute-start | bytes 1572872 | tf_op jit(solution)/shard_map/ppermute | solution.py:295
  184.8 4.3 %shard_map.58.near = f32[16,2048]{1,0:T(8,128)S(1)} custom-call(s32[4]{0:T(128)S(1)} %pad_add_fusion.idx, f32[512,512]{1,0:T(8,128)S(1)} %collective-permute-done.21.up.refs_0_, f32[512,512]{1,0:T(8,128)S(1)} %collective-permute-done.22.down.refs_1_, f32[512,512]{1,0:T(8,128)S(1)} %constant_dynamic-update-slice_fusion.own.refs_2_), custom_call_target="tpu_custom_call" | custom-call | flops 10000000 | bytes 1048576 | tf_op jit(solution)/shard_map/pallas_call | solution.py:360
  189.1 2.5 %shard_map.59 = f32[16,2048]{1,0:T(8,128)} custom-call(s32[4]{0:T(128)S(1)} %pad_add_fusion.idx, f32[16,2048]{1,0:T(8,128)S(1)} %shard_map.58.near, f32[256,512]{1,0:T(8,128)S(1)} %collective-permute-done.23.low, f32[256,512]{1,0:T(8,128)S(1)} %collective-permute-done.24.up), custom_call_target="tpu_custom_call" | custom-call | flops 10000000 | bytes 1048576 | tf_op jit(solution)/shard_map/pallas_call | solution.py:363
  (86 shorter events, 24.8 us)
Async XLA Ops:
  0.6 37.6 %copy-start = (f32[512,16]{0,1:T(8,128)S(1)}, f32[512,16]{0,1:T(8,128)}, u32[]{:S(2)}) copy-start(f32[512,16]{0,1:T(8,128)} %param.3) | copy-start | bytes 98308
  0.6 6.3 %collective-permute-start.2 = (f32[64,512]{1,0:T(8,128)}, f32[64,512]{1,0:T(8,128)S(1)}, u32[]{:S(2)}, u32[]{:S(2)}) collective-permute-start(f32[64,512]{1,0:T(8,128)} %bitcast.56), channel_id=1, source_target_pairs={{0,128},{64,192},{128,0},{192,64},{1,129},{65,193},{129,1},{193,65... | collective-permute-start | bytes 393224 | tf_op jit(solution)/shard_map/ppermute | solution.py:259
  4.3 7.5 %collective-permute-start.3 = (f32[64,512]{1,0:T(8,128)}, f32[64,512]{1,0:T(8,128)S(1)}, u32[]{:S(2)}, u32[]{:S(2)}) collective-permute-start(f32[64,512]{1,0:T(8,128)} %bitcast.57), channel_id=1, source_target_pairs={{0,64},{64,128},{128,192},{192,0},{1,65},{65,129},{129,193},{193,1... | collective-permute-start | bytes 393224 | tf_op jit(solution)/shard_map/ppermute | solution.py:259
  4.6 7.2 %collective-permute-start.1 = (f32[64,512]{1,0:T(8,128)}, f32[64,512]{1,0:T(8,128)S(1)}, u32[]{:S(2)}, u32[]{:S(2)}) collective-permute-start(f32[64,512]{1,0:T(8,128)} %bitcast.58), channel_id=1, source_target_pairs={{0,192},{64,0},{128,64},{192,128},{1,193},{65,1},{129,65},{193,129... | collective-permute-start | bytes 393224 | tf_op jit(solution)/shard_map/ppermute | solution.py:259
  12.8 6.0 %collective-permute-start.4 = (f32[4,64,512]{2,1,0:T(8,128)S(1)}, f32[4,64,512]{2,1,0:T(8,128)S(1)}, u32[]{:S(2)}, u32[]{:S(2)}) collective-permute-start(f32[4,64,512]{2,1,0:T(8,128)S(1)} %get-tuple-element.36), channel_id=1, source_target_pairs={{0,32},{32,0},{1,33},{33,1},{2,34},{34,2},{3,35},{35,3},{4,36},{36... | collective-permute-start | bytes 1572872 | tf_op jit(solution)/shard_map/ppermute | solution.py:295
  14.2 2.2 %copy-start.4 = (f32[2048,512]{1,0:T(8,128)S(1)}, f32[2048,512]{1,0:T(8,128)}, u32[]{:S(2)}) copy-start(f32[2048,512]{1,0:T(8,128)} %w.1) | copy-start | bytes 12582916
  20.7 14.5 %collective-permute-start.5 = (f32[256,512]{1,0:T(8,128)S(1)}, f32[256,512]{1,0:T(8,128)S(1)}, u32[]{:S(2)}, u32[]{:S(2)}) collective-permute-start(f32[256,512]{1,0:T(8,128)S(1)} %get-tuple-element.20), channel_id=1, source_target_pairs={{0,1},{1,2},{2,3},{3,0},{4,5},{5,6},{6,7},{7,4},{8,9},{9,10},{10,1... | collective-permute-start | bytes 1572872 | tf_op jit(solution)/shard_map/ppermute | solution.py:254
  21.4 13.8 %collective-permute-start.6 = (f32[256,512]{1,0:T(8,128)S(1)}, f32[256,512]{1,0:T(8,128)S(1)}, u32[]{:S(2)}, u32[]{:S(2)}) collective-permute-start(f32[256,512]{1,0:T(8,128)S(1)} %get-tuple-element.21), channel_id=1, source_target_pairs={{0,3},{1,0},{2,1},{3,2},{4,7},{5,4},{6,5},{7,6},{8,11},{9,8},{10,9... | collective-permute-start | bytes 1572872 | tf_op jit(solution)/shard_map/ppermute | solution.py:254
  35.4 51.9 %collective-permute-start.7 = (f32[512,512]{1,0:T(8,128)S(1)}, f32[512,512]{1,0:T(8,128)S(1)}, u32[]{:S(2)}, u32[]{:S(2)}) collective-permute-start(f32[512,512]{1,0:T(8,128)S(1)} %get-tuple-element.22), channel_id=1, source_target_pairs={{0,1},{1,2},{2,3},{3,0},{4,5},{5,6},{6,7},{7,4},{8,9},{9,10},{10,1... | collective-permute-start | bytes 3145736 | tf_op jit(solution)/shard_map/ppermute | solution.py:254
  36.0 51.3 %collective-permute-start.8 = (f32[512,512]{1,0:T(8,128)S(1)}, f32[512,512]{1,0:T(8,128)S(1)}, u32[]{:S(2)}, u32[]{:S(2)}) collective-permute-start(f32[512,512]{1,0:T(8,128)S(1)} %get-tuple-element.23), channel_id=1, source_target_pairs={{0,3},{1,0},{2,1},{3,2},{4,7},{5,4},{6,5},{7,6},{8,11},{9,8},{10,9... | collective-permute-start | bytes 3145736 | tf_op jit(solution)/shard_map/ppermute | solution.py:254
  83.3 6.0 %collective-permute-start = (f32[512,256]{1,0:T(8,128)S(1)}, f32[512,256]{1,0:T(8,128)S(1)}, u32[]{:S(2)}, u32[]{:S(2)}) collective-permute-start(f32[512,256]{1,0:T(8,128)S(1)} %bitcast.50), channel_id=1, source_target_pairs={{0,32},{32,0},{1,33},{33,1},{2,34},{34,2},{3,35},{35,3},{4,36},{36... | collective-permute-start | bytes 1572872 | tf_op jit(solution)/shard_map/ppermute | solution.py:295
  87.7 7.9 %collective-permute-start.10 = (f32[128,512]{1,0:T(8,128)S(1)}, f32[128,512]{1,0:T(8,128)S(1)}, u32[]{:S(2)}, u32[]{:S(2)}) collective-permute-start(f32[128,512]{1,0:T(8,128)S(1)} %get-tuple-element.30), channel_id=1, source_target_pairs={{0,28},{4,0},{8,4},{12,8},{16,12},{20,16},{24,20},{28,24},{1,29},{... | collective-permute-start | bytes 786440 | tf_op jit(solution)/shard_map/ppermute | solution.py:254
  87.8 9.3 %collective-permute-start.9 = (f32[128,512]{1,0:T(8,128)S(1)}, f32[128,512]{1,0:T(8,128)S(1)}, u32[]{:S(2)}, u32[]{:S(2)}) collective-permute-start(f32[128,512]{1,0:T(8,128)S(1)} %get-tuple-element.31), channel_id=1, source_target_pairs={{0,4},{4,8},{8,12},{12,16},{16,20},{20,24},{24,28},{28,0},{1,5},{5... | collective-permute-start | bytes 786440 | tf_op jit(solution)/shard_map/ppermute | solution.py:254
  97.3 5.6 %collective-permute-start.11 = (f32[32,512]{1,0:T(8,128)S(1)}, f32[32,512]{1,0:T(8,128)S(1)}, u32[]{:S(2)}, u32[]{:S(2)}) collective-permute-start(f32[32,512]{1,0:T(8,128)S(1)} %get-tuple-element.41), channel_id=1, source_target_pairs={{0,8},{4,12},{8,16},{12,20},{16,24},{20,28},{24,0},{28,4},{1,9},{5... | collective-permute-start | bytes 196616 | tf_op jit(solution)/shard_map/ppermute | solution.py:254
  97.4 5.5 %collective-permute-start.12 = (f32[32,512]{1,0:T(8,128)S(1)}, f32[32,512]{1,0:T(8,128)S(1)}, u32[]{:S(2)}, u32[]{:S(2)}) collective-permute-start(f32[32,512]{1,0:T(8,128)S(1)} %get-tuple-element.37), channel_id=1, source_target_pairs={{0,24},{4,28},{8,0},{12,4},{16,8},{20,12},{24,16},{28,20},{1,25},{... | collective-permute-start | bytes 196616 | tf_op jit(solution)/shard_map/ppermute | solution.py:254
  102.9 9.4 %collective-permute-start.13 = (f32[64,512]{1,0:T(8,128)S(1)}, f32[64,512]{1,0:T(8,128)S(1)}, u32[]{:S(2)}, u32[]{:S(2)}) collective-permute-start(f32[64,512]{1,0:T(8,128)S(1)} %get-tuple-element.26), channel_id=1, source_target_pairs={{0,8},{4,12},{8,16},{12,20},{16,24},{20,28},{24,0},{28,4},{1,9},{5... | collective-permute-start | bytes 393224 | tf_op jit(solution)/shard_map/ppermute | solution.py:254
  104.9 7.4 %collective-permute-start.14 = (f32[64,512]{1,0:T(8,128)S(1)}, f32[64,512]{1,0:T(8,128)S(1)}, u32[]{:S(2)}, u32[]{:S(2)}) collective-permute-start(f32[64,512]{1,0:T(8,128)S(1)} %get-tuple-element.27), channel_id=1, source_target_pairs={{0,24},{4,28},{8,0},{12,4},{16,8},{20,12},{24,16},{28,20},{1,25},{... | collective-permute-start | bytes 393224 | tf_op jit(solution)/shard_map/ppermute | solution.py:254
  112.3 44.1 %copy-start.3 = (f32[2048,512]{1,0:T(8,128)S(1)}, f32[2048,512]{1,0:T(8,128)}, u32[]{:S(2)}) copy-start(f32[2048,512]{1,0:T(8,128)} %copy-done.1) | copy-start | bytes 12582916
  113.0 8.4 %collective-permute-start.15 = (f32[64,512]{1,0:T(8,128)S(1)}, f32[64,512]{1,0:T(8,128)S(1)}, u32[]{:S(2)}, u32[]{:S(2)}) collective-permute-start(f32[64,512]{1,0:T(8,128)S(1)} %shard_map.57), channel_id=1, source_target_pairs={{0,24},{4,28},{8,0},{12,4},{16,8},{20,12},{24,16},{28,20},{1,25},{... | collective-permute-start | bytes 393224 | tf_op jit(solution)/shard_map/ppermute | solution.py:254
  115.4 5.9 %collective-permute-start.16 = (f32[64,512]{1,0:T(8,128)S(1)}, f32[64,512]{1,0:T(8,128)S(1)}, u32[]{:S(2)}, u32[]{:S(2)}) collective-permute-start(f32[64,512]{1,0:T(8,128)S(1)} %shard_map.57), channel_id=1, source_target_pairs={{0,8},{4,12},{8,16},{12,20},{16,24},{20,28},{24,0},{28,4},{1,9},{5... | collective-permute-start | bytes 393224 | tf_op jit(solution)/shard_map/ppermute | solution.py:254
  121.3 5.8 %collective-permute-start.17 = (f32[32,512]{1,0:T(8,128)S(1)}, f32[32,512]{1,0:T(8,128)S(1)}, u32[]{:S(2)}, u32[]{:S(2)}) collective-permute-start(f32[32,512]{1,0:T(8,128)S(1)} %get-tuple-element.50), channel_id=1, source_target_pairs={{0,8},{4,12},{8,16},{12,20},{16,24},{20,28},{24,0},{28,4},{1,9},{5... | collective-permute-start | bytes 196616 | tf_op jit(solution)/shard_map/ppermute | solution.py:254
  121.5 5.8 %collective-permute-start.19 = (f32[32,512]{1,0:T(8,128)S(1)}, f32[32,512]{1,0:T(8,128)S(1)}, u32[]{:S(2)}, u32[]{:S(2)}) collective-permute-start(f32[32,512]{1,0:T(8,128)S(1)} %get-tuple-element.47), channel_id=1, source_target_pairs={{0,24},{4,28},{8,0},{12,4},{16,8},{20,12},{24,16},{28,20},{1,25},{... | collective-permute-start | bytes 196616 | tf_op jit(solution)/shard_map/ppermute | solution.py:254
  127.2 6.5 %collective-permute-start.18 = (f32[128,512]{1,0:T(8,128)S(1)}, f32[128,512]{1,0:T(8,128)S(1)}, u32[]{:S(2)}, u32[]{:S(2)}) collective-permute-start(f32[128,512]{1,0:T(8,128)S(1)} %pad_maximum_fusion.2), channel_id=1, source_target_pairs={{0,28},{4,0},{8,4},{12,8},{16,12},{20,16},{24,20},{28,24},{1,29},{... | collective-permute-start | bytes 786440 | tf_op jit(solution)/shard_map/ppermute | solution.py:254
  127.3 7.9 %collective-permute-start.20 = (f32[128,512]{1,0:T(8,128)S(1)}, f32[128,512]{1,0:T(8,128)S(1)}, u32[]{:S(2)}, u32[]{:S(2)}) collective-permute-start(f32[128,512]{1,0:T(8,128)S(1)} %pad_maximum_fusion.3), channel_id=1, source_target_pairs={{0,4},{4,8},{8,12},{12,16},{16,20},{20,24},{24,28},{28,0},{1,5},{5... | collective-permute-start | bytes 786440 | tf_op jit(solution)/shard_map/ppermute | solution.py:254
  135.4 18.1 %collective-permute-start.22 = (f32[512,512]{1,0:T(8,128)S(1)}, f32[512,512]{1,0:T(8,128)S(1)}, u32[]{:S(2)}, u32[]{:S(2)}) collective-permute-start(f32[512,512]{1,0:T(8,128)S(1)} %constant_dynamic-update-slice_fusion.own.refs_2_), channel_id=1, source_target_pairs={{0,1},{1,2},{2,3},{3,0},{4,5},{5,6},{6,7},{7,4},{8,9},{9,10},{10,1... | collective-permute-start | bytes 3145736 | tf_op jit(solution)/shard_map/ppermute | solution.py:254
  136.1 17.5 %collective-permute-start.21 = (f32[512,512]{1,0:T(8,128)S(1)}, f32[512,512]{1,0:T(8,128)S(1)}, u32[]{:S(2)}, u32[]{:S(2)}) collective-permute-start(f32[512,512]{1,0:T(8,128)S(1)} %constant_dynamic-update-slice_fusion.own.refs_2_), channel_id=1, source_target_pairs={{0,3},{1,0},{2,1},{3,2},{4,7},{5,4},{6,5},{7,6},{8,11},{9,8},{10,9... | collective-permute-start | bytes 3145736 | tf_op jit(solution)/shard_map/ppermute | solution.py:254
  153.5 13.9 %collective-permute-start.23 = (f32[256,512]{1,0:T(8,128)S(1)}, f32[256,512]{1,0:T(8,128)S(1)}, u32[]{:S(2)}, u32[]{:S(2)}) collective-permute-start(f32[256,512]{1,0:T(8,128)S(1)} %slice.128), channel_id=1, source_target_pairs={{0,1},{1,2},{2,3},{3,0},{4,5},{5,6},{6,7},{7,4},{8,9},{9,10},{10,1... | collective-permute-start | bytes 1572872 | tf_op jit(solution)/shard_map/ppermute | solution.py:254
  153.6 13.8 %collective-permute-start.24 = (f32[256,512]{1,0:T(8,128)S(1)}, f32[256,512]{1,0:T(8,128)S(1)}, u32[]{:S(2)}, u32[]{:S(2)}) collective-permute-start(f32[256,512]{1,0:T(8,128)S(1)} %slice.129), channel_id=1, source_target_pairs={{0,3},{1,0},{2,1},{3,2},{4,7},{5,4},{6,5},{7,6},{8,11},{9,8},{10,9... | collective-permute-start | bytes 1572872 | tf_op jit(solution)/shard_map/ppermute | solution.py:254
  168.7 11.8 %collective-permute-start.25 = (f32[4,64,512]{2,1,0:T(8,128)S(1)}, f32[4,64,512]{2,1,0:T(8,128)S(1)}, u32[]{:S(2)}, u32[]{:S(2)}) collective-permute-start(f32[4,64,512]{2,1,0:T(8,128)S(1)} %slice_bitcast_fusion), channel_id=1, source_target_pairs={{0,32},{32,0},{1,33},{33,1},{2,34},{34,2},{3,35},{35,3},{4,36},{36... | collective-permute-start | bytes 1572872 | tf_op jit(solution)/shard_map/ppermute | solution.py:295
  180.6 11.0 %collective-permute-start.26 = (f32[64,512]{1,0:T(8,128)S(1)}, f32[64,512]{1,0:T(8,128)S(1)}, u32[]{:S(2)}, u32[]{:S(2)}) collective-permute-start(f32[64,512]{1,0:T(8,128)S(1)} %get-tuple-element.32), channel_id=1, source_target_pairs={{0,64},{64,128},{128,192},{192,0},{1,65},{65,129},{129,193},{193,1... | collective-permute-start | bytes 393224 | tf_op jit(solution)/shard_map/ppermute | solution.py:259
  182.4 9.2 %collective-permute-start.27 = (f32[64,512]{1,0:T(8,128)S(1)}, f32[64,512]{1,0:T(8,128)S(1)}, u32[]{:S(2)}, u32[]{:S(2)}) collective-permute-start(f32[64,512]{1,0:T(8,128)S(1)} %get-tuple-element.34), channel_id=1, source_target_pairs={{0,192},{64,0},{128,64},{192,128},{1,193},{65,1},{129,65},{193,129... | collective-permute-start | bytes 393224 | tf_op jit(solution)/shard_map/ppermute | solution.py:259
  183.7 7.8 %collective-permute-start.28 = (f32[64,512]{1,0:T(8,128)S(1)}, f32[64,512]{1,0:T(8,128)S(1)}, u32[]{:S(2)}, u32[]{:S(2)}) collective-permute-start(f32[64,512]{1,0:T(8,128)S(1)} %get-tuple-element.33), channel_id=1, source_target_pairs={{0,128},{64,192},{128,0},{192,64},{1,129},{65,193},{129,1},{193,65... | collective-permute-start | bytes 393224 | tf_op jit(solution)/shard_map/ppermute | solution.py:259
  (2 other events, 4.2 us)

commit v2 on v1

--- a/solution.py
+++ b/solution.py
@@ -197,15 +197,11 @@
 
 
 def near_kernel(w, *refs):
-    chunks, out = refs[:3], refs[3]
+    chunks, out = refs[:-1], refs[-1]
     out[...] = jnp.zeros_like(out)
     for k, chunk in enumerate(chunks):
-
-        @pl.loop(0, CHUNK // STEP)
-        def _(i):
-            rows = pl.ds(pl.multiple_of(CHUNK * (k + 1) + i * STEP, STEP), STEP)
-            source = pl.ds(pl.multiple_of(i * STEP, STEP), STEP)
-            out[...] += dot_three(halves(chunk[source, :]), halves(w[rows, :]), TN)
+        first = CHUNK + k * STEP
+        out[...] += dot_three(halves(chunk[...]), halves(w[first : first + STEP, :]), TN)
 
 
 def scale_kernel(x11, a0, a1, a2, out):
@@ -235,9 +231,10 @@
         yield pl.ds(pl.multiple_of(base, CHUNK), CHUNK), held[...].T[:16, :]
 
 
-def near_columns_kernel(idx, up, down, own, out, held):
+def near_columns_kernel(idx, *refs):
+    out, held = refs[6:]
     out[...] = jnp.zeros_like(out)
-    for place, value in take_columns(idx, ORDER[1:], ((up,), (down,), (own,)), held):
+    for place, value in take_columns(idx, ORDER[1:], (refs[0:2], refs[2:4], refs[4:6]), held):
         out[:, place] = value
 
 
@@ -279,7 +276,10 @@
     right, left = ring(axis, stride)
     half = own.shape[0] // 2
     a, b = right(own), left(own)
-    return {0: own, 1: b, 3: a}, right(a[:half]), left(b[half:])
+    a, b = lax.optimization_barrier((a, b))
+    low, up = right(a[:half]), left(b[half:])
+    low, up = lax.optimization_barrier((low, up))
+    return {0: own, 1: b, 3: a}, low, up
 
 
 def dot_high(a, b, dims):
@@ -349,17 +349,20 @@
     near, low, up = gather_of_four(own, "z", 2)
     a = jnp.concatenate([near[0][:HALF], near[1][:HALF], low, near[3][:HALF]], axis=0)
     b = jnp.concatenate([near[0][HALF:], near[1][HALF:], up, near[3][HALF:]], axis=0)
-    own = jnp.concatenate([left(a), right(b), a, b], axis=0)
-    chunks, far_low, far_up = gather_of_four(own, "y")
+    even = jnp.concatenate([a, b], axis=0)
+    right_of_y, left_of_y = ring("y")
+    down_even, up_even = right_of_y(even), left_of_y(even)
+    odd = jnp.concatenate([left(a), right(b)], axis=0)
+    down_odd, up_odd = right_of_y(odd), left_of_y(odd)
+    far_up, far_low = left_of_y(up_even), right_of_y(down_odd)
+    near = [up_odd, up_even, down_odd, down_even, odd, even]
     total = call(
-        near_kernel, shape((BLK, BLK), f32), 4, 6 * (ROWS - CHUNK) * BLK * BLK, smem=False, mib=14
-    )(w, *[chunks[dy] for dy in ORDER[1:]])
+        near_kernel, shape((BLK, BLK), f32), 7, 6 * (ROWS - CHUNK) * BLK * BLK, smem=False, mib=14
+    )(w, *near)
     update = total + dot_high(jnp.concatenate([far_low, far_up], axis=0), w[:CHUNK], TN)
     held = [pltpu.VMEM((CHUNK, 128), f32)]
     strip = shape((16, ROWS), f32)
-    columns = call(near_columns_kernel, strip, 3, 10**7, scratch=held)(
-        idx, *[chunks[dy] for dy in ORDER[1:]]
-    )
+    columns = call(near_columns_kernel, strip, 6, 10**7, scratch=held)(idx, *near)
     columns = call(far_columns_kernel, strip, 3, 10**7, scratch=held)(idx, columns, far_low, far_up)
 
     blocks = update.reshape(NX, NC, 64, BLK)

time: 192 us -> 189 us (0.984)
  waiting for transfers between devices: 55.1 us -> 51.8 us
    ppermute x10 -> x11, waiting for transfers between devices: 41 us -> 33.6 us  [ring(): lax.ppermute(v, axis, right)]
    ppermute x10 -> x11, waiting for transfers between devices: 7.76 us -> 11.9 us  [ring(): lax.ppermute(v, axis, left)]
    ppermute x10 -> x11, starting transfers between devices: 20.5 us -> 22.6 us  [ring(): lax.ppermute(v, axis, left)]
    ppermute x10 -> x11, starting transfers between devices: 7.59 us -> 8.68 us  [ring(): lax.ppermute(v, axis, right)]
    unnamed x19 -> x18, local copies, waits for them, and re-layouts: 5.22 us -> 5.21 us
  transfers between devices with their start and end apart: 29 -> 31, of which waited for: 12 -> 15; matrix products, arithmetic and copies ran while one was open for 0% -> 0% of each run, Pallas kernels for 13% -> 13%
where the time goes in v2:
time: 189 us
  starting transfers between devices  56 us (30%)
  waiting for transfers between devices  51.8 us (27%)
  blocking collectives  45.1 us (24%)
  Pallas kernels  26.3 us (14%)
  local copies, waits for them, and re-layouts  5.5 us (3%)
  other arithmetic  2.48 us (1%)
    all_to_all x2, blocking collectives, steps(): part = lax.all_to_all(copies, axis, split_axis=0, concat_axis=0, tiled=True)  45.1 us
    ppermute x11, waiting for transfers between devices, ring(): lax.ppermute(v, axis, right)  33.6 us
    ppermute x11, starting transfers between devices, ring(): lax.ppermute(v, axis, left)  22.6 us
    ppermute x3, starting transfers between devices, steps(): swap = lambda v: lax.ppermute(v, 'core', [(0, 1), (1, 0)])  14.1 us
    ppermute x11, waiting for transfers between devices, ring(): lax.ppermute(v, axis, left)  11.9 us
    ppermute x6, starting transfers between devices, shifted(): return lax.ppermute(value, axis, [(i, (i + hops) % n) for i in range(n)])  10.6 us
    ppermute x11, starting transfers between devices, ring(): lax.ppermute(v, axis, right)  8.68 us
    pallas_call x1, Pallas kernels, steps(): call(inverse_kernel, square, 2, 10 ** 9, scratch=[pltpu.VMEM((BLK, BLK),...  5.6 us
  transfers between devices with their start and end apart: 31, of which 15 were waited for; matrix products, arithmetic and copies ran while one was open for 0% of the time, Pallas kernels for 13%

profile of v2, /device:TPU:1, one launch (start us, length us, event | category | flops | bytes accessed | tf_op | source)
XLA Modules:
  0.0 189.1 jit_solution(2516693633456905930)
XLA Ops:
  0.6 3.6 %collective-permute-start.2 = (f32[64,512]{1,0:T(8,128)}, f32[64,512]{1,0:T(8,128)S(1)}, u32[]{:S(2)}, u32[]{:S(2)}) collective-permute-start(f32[64,512]{1,0:T(8,128)} %bitcast.56), channel_id=1, source_target_pairs={{0,128},{64,192},{128,0},{192,64},{1,129},{65,193},{129,1},{193,65... | collective-permute-start | bytes 393224 | tf_op jit(solution)/shard_map/ppermute | solution.py:256
  4.6 2.4 %collective-permute-start.1 = (f32[64,512]{1,0:T(8,128)}, f32[64,512]{1,0:T(8,128)S(1)}, u32[]{:S(2)}, u32[]{:S(2)}) collective-permute-start(f32[64,512]{1,0:T(8,128)} %bitcast.58), channel_id=1, source_target_pairs={{0,192},{64,0},{128,64},{192,128},{1,193},{65,1},{129,65},{193,129... | collective-permute-start | bytes 393224 | tf_op jit(solution)/shard_map/ppermute | solution.py:256
  7.0 4.8 %collective-permute-done.3 = f32[64,512]{1,0:T(8,128)S(1)} collective-permute-done((f32[64,512]{1,0:T(8,128)}, f32[64,512]{1,0:T(8,128)S(1)}, u32[]{:S(2)}, u32[]{:S(2)}) %collective-permute-start.3) | collective-permute-done | bytes 131104 | tf_op jit(solution)/shard_map/ppermute | solution.py:256
  14.2 2.2 %copy-done.4 = f32[2048,512]{1,0:T(8,128)S(1)} copy-done((f32[2048,512]{1,0:T(8,128)S(1)}, f32[2048,512]{1,0:T(8,128)}, u32[]{:S(2)}) %copy-start.4) | copy-done | bytes 4194328
  16.4 2.3 %shard_map.52.w = f32[2048,512]{1,0:T(8,128)S(1)} custom-call(s32[4]{0:T(128)S(1)} %pad_add_fusion.idx, f32[2048,512]{1,0:T(8,128)S(1)} %copy-done.4), custom_call_target="tpu_custom_call" | custom-call | flops 100000000 | bytes 1048576 | tf_op jit(solution)/shard_map/pallas_call | solution.py:320
  23.4 2.2 %copy-done.2 = f32[2048,512]{1,0:T(8,128)S(1)} copy-done((f32[2048,512]{1,0:T(8,128)S(1)}, f32[2048,512]{1,0:T(8,128)}, u32[]{:S(2)}) %copy-start.2) | copy-done | bytes 4194328
  25.6 3.8 %shard_map.53 = (f32[512,512]{1,0:T(8,128)S(1)}, f32[512,512]{1,0:T(8,128)S(1)}, f32[512,512]{1,0:T(8,128)S(1)}) custom-call(f32[512,512]{1,0:T(8,128)S(1)} %bitcast.49, f32[2048,512]{1,0:T(8,128)S(1)} %copy-done.2), custom_call_target="tpu_custom_call" | custom-call | flops 2415919104 | bytes 1048576 | tf_op jit(solution)/shard_map/pallas_call | solution.py:324
  29.4 5.9 %collective-permute-done.5.a = f32[256,512]{1,0:T(8,128)S(1)} collective-permute-done((f32[256,512]{1,0:T(8,128)S(1)}, f32[256,512]{1,0:T(8,128)S(1)}, u32[]{:S(2)}, u32[]{:S(2)}) %collective-permute-start.5) | collective-permute-done | bytes 524320 | tf_op jit(solution)/shard_map/ppermute | solution.py:251
  36.0 2.2 %collective-permute-start.8 = (f32[512,512]{1,0:T(8,128)S(1)}, f32[512,512]{1,0:T(8,128)S(1)}, u32[]{:S(2)}, u32[]{:S(2)}) collective-permute-start(f32[512,512]{1,0:T(8,128)S(1)} %get-tuple-element.27), channel_id=1, source_target_pairs={{0,3},{1,0},{2,1},{3,2},{4,7},{5,4},{6,5},{7,6},{8,11},{9,8},{10,9... | collective-permute-start | bytes 3145736 | tf_op jit(solution)/shard_map/ppermute | solution.py:251
  38.2 23.2 %all_to_all.10 = f32[4,16,256]{2,1,0:T(8,128)S(1)} all-to-all(f32[4,16,256]{2,1,0:T(8,128)S(1)} %broadcast_in_dim.6), channel_id=1, replica_groups=mesh['x'=4,'core'=2,'z'=8,'y'=4] {'y'}, dimensions={0} | all-to-all | bytes 131072 | tf_op jit(solution)/shard_map/all_to_all | solution.py:306
  61.5 21.8 %all_to_all.11 = f32[8,64,256]{2,1,0:T(8,128)S(1)} all-to-all(f32[8,64,256]{2,1,0:T(8,128)S(1)} %broadcast_in_dim.7), channel_id=1, replica_groups=mesh['x'=4,'core'=2,'z'=8,'y'=4] {'z'}, dimensions={0} | all-to-all | bytes 1048576 | tf_op jit(solution)/shard_map/all_to_all | solution.py:306
  83.3 4.0 %collective-permute-start = (f32[512,256]{1,0:T(8,128)S(1)}, f32[512,256]{1,0:T(8,128)S(1)}, u32[]{:S(2)}, u32[]{:S(2)}) collective-permute-start(f32[512,256]{1,0:T(8,128)S(1)} %bitcast.50), channel_id=1, source_target_pairs={{0,32},{32,0},{1,33},{33,1},{2,34},{34,2},{3,35},{35,3},{4,36},{36... | collective-permute-start | bytes 1572872 | tf_op jit(solution)/shard_map/ppermute | solution.py:295
  89.3 3.3 %shard_map.50 = (f32[512,512]{1,0:T(8,128)S(1)}, f32[512,512]{1,0:T(8,128)S(1)}) custom-call(s32[4]{0:T(128)S(1)} %pad_add_fusion.idx, f32[512,256]{1,0:T(8,128)S(1)} %bitcast.51, f32[512,256]{1,0:T(8,128)S(1)} %collective-permute-done.other), custom_call_target="tpu_custom_call" | custom-call | flops 1000000000 | bytes 1048576 | tf_op jit(solution)/shard_map/pallas_call | solution.py:311
  92.6 3.1 %collective-permute-done.10 = f32[128,512]{1,0:T(8,128)S(1)} collective-permute-done((f32[128,512]{1,0:T(8,128)S(1)}, f32[128,512]{1,0:T(8,128)S(1)}, u32[]{:S(2)}, u32[]{:S(2)}) %collective-permute-start.10) | collective-permute-done | bytes 262176 | tf_op jit(solution)/shard_map/ppermute | solution.py:251
  97.4 3.6 %collective-permute-start.12 = (f32[32,512]{1,0:T(8,128)S(1)}, f32[32,512]{1,0:T(8,128)S(1)}, u32[]{:S(2)}, u32[]{:S(2)}) collective-permute-start(f32[32,512]{1,0:T(8,128)S(1)} %get-tuple-element.45), channel_id=1, source_target_pairs={{0,24},{4,28},{8,0},{12,4},{16,8},{20,12},{24,16},{28,20},{1,25},{... | collective-permute-start | bytes 196616 | tf_op jit(solution)/shard_map/ppermute | solution.py:251
  102.9 2.1 %collective-permute-start.13 = (f32[64,512]{1,0:T(8,128)S(1)}, f32[64,512]{1,0:T(8,128)S(1)}, u32[]{:S(2)}, u32[]{:S(2)}) collective-permute-start(f32[64,512]{1,0:T(8,128)S(1)} %get-tuple-element.30), channel_id=1, source_target_pairs={{0,8},{4,12},{8,16},{12,20},{16,24},{20,28},{24,0},{28,4},{1,9},{5... | collective-permute-start | bytes 393224 | tf_op jit(solution)/shard_map/ppermute | solution.py:251
  106.7 5.6 %shard_map.51.x11 = f32[512,512]{1,0:T(8,128)S(1)} custom-call(s32[4]{0:T(128)S(1)} %pad_add_fusion.idx, f32[512,512]{1,0:T(8,128)S(1)} %get-tuple-element.19.u, f32[512,512]{1,0:T(8,128)S(1)} %get-tuple-element.20.diagonal), custom_call_target="tpu_custom_call" | custom-call | flops 1000000000 | bytes 1048576 | tf_op jit(solution)/shard_map/pallas_call | solution.py:312
  114.3 2.4 %collective-permute-start.16 = (f32[64,512]{1,0:T(8,128)S(1)}, f32[64,512]{1,0:T(8,128)S(1)}, u32[]{:S(2)}, u32[]{:S(2)}) collective-permute-start(f32[64,512]{1,0:T(8,128)S(1)} %shard_map.57), channel_id=1, source_target_pairs={{0,24},{4,28},{8,0},{12,4},{16,8},{20,12},{24,16},{28,20},{1,25},{... | collective-permute-start | bytes 393224 | tf_op jit(solution)/shard_map/ppermute | solution.py:251
  116.7 3.0 %collective-permute-done.15 = f32[64,512]{1,0:T(8,128)S(1)} collective-permute-done((f32[64,512]{1,0:T(8,128)S(1)}, f32[64,512]{1,0:T(8,128)S(1)}, u32[]{:S(2)}, u32[]{:S(2)}) %collective-permute-start.15) | collective-permute-done | bytes 131104 | tf_op jit(solution)/shard_map/ppermute | solution.py:251
  119.7 4.1 %collective-permute-start.18 = (f32[32,512]{1,0:T(8,128)S(1)}, f32[32,512]{1,0:T(8,128)S(1)}, u32[]{:S(2)}, u32[]{:S(2)}) collective-permute-start(f32[32,512]{1,0:T(8,128)S(1)} %get-tuple-element.61), channel_id=1, source_target_pairs={{0,24},{4,28},{8,0},{12,4},{16,8},{20,12},{24,16},{28,20},{1,25},{... | collective-permute-start | bytes 196616 | tf_op jit(solution)/shard_map/ppermute | solution.py:251
  125.6 3.3 %collective-permute-done.17 = f32[32,512]{1,0:T(8,128)S(1)} collective-permute-done((f32[32,512]{1,0:T(8,128)S(1)}, f32[32,512]{1,0:T(8,128)S(1)}, u32[]{:S(2)}, u32[]{:S(2)}) %collective-permute-start.17) | collective-permute-done | bytes 65568 | tf_op jit(solution)/shard_map/ppermute | solution.py:251
  130.7 2.0 %collective-permute-start.22 = (f32[256,512]{1,0:T(8,128)S(1)}, f32[256,512]{1,0:T(8,128)S(1)}, u32[]{:S(2)}, u32[]{:S(2)}) collective-permute-start(f32[256,512]{1,0:T(8,128)S(1)} %get-tuple-element.53.refs_5_), channel_id=1, source_target_pairs={{0,3},{1,0},{2,1},{3,2},{4,7},{5,4},{6,5},{7,6},{8,11},{9,8},{10,9... | collective-permute-start | bytes 1572872 | tf_op jit(solution)/shard_map/ppermute | solution.py:251
  137.5 2.5 %collective-permute-start.21 = (f32[256,512]{1,0:T(8,128)S(1)}, f32[256,512]{1,0:T(8,128)S(1)}, u32[]{:S(2)}, u32[]{:S(2)}) collective-permute-start(f32[256,512]{1,0:T(8,128)S(1)} %constant_dynamic-update-slice_fusion.refs_4_), channel_id=1, source_target_pairs={{0,3},{1,0},{2,1},{3,2},{4,7},{5,4},{6,5},{7,6},{8,11},{9,8},{10,9... | collective-permute-start | bytes 1572872 | tf_op jit(solution)/shard_map/ppermute | solution.py:251
  140.0 2.1 %collective-permute-start.26 = (f32[256,512]{1,0:T(8,128)S(1)}, f32[256,512]{1,0:T(8,128)S(1)}, u32[]{:S(2)}, u32[]{:S(2)}) collective-permute-start(f32[256,512]{1,0:T(8,128)S(1)} %collective-permute-done.22.refs_1_), channel_id=1, source_target_pairs={{0,3},{1,0},{2,1},{3,2},{4,7},{5,4},{6,5},{7,6},{8,11},{9,8},{10,9... | collective-permute-start | bytes 1572872 | tf_op jit(solution)/shard_map/ppermute | solution.py:251
  142.0 3.8 %collective-permute-done.23.refs_2_ = f32[256,512]{1,0:T(8,128)S(1)} collective-permute-done((f32[256,512]{1,0:T(8,128)S(1)}, f32[256,512]{1,0:T(8,128)S(1)}, u32[]{:S(2)}, u32[]{:S(2)}) %collective-permute-start.23) | collective-permute-done | bytes 524320 | tf_op jit(solution)/shard_map/ppermute | solution.py:251
  145.8 8.9 %collective-permute-done.24.refs_3_ = f32[256,512]{1,0:T(8,128)S(1)} collective-permute-done((f32[256,512]{1,0:T(8,128)S(1)}, f32[256,512]{1,0:T(8,128)S(1)}, u32[]{:S(2)}, u32[]{:S(2)}) %collective-permute-start.24) | collective-permute-done | bytes 524320 | tf_op jit(solution)/shard_map/ppermute | solution.py:251
  154.7 2.6 %shard_map.60 = f32[512,512]{1,0:T(8,128)S(1)} custom-call(f32[2048,512]{1,0:T(8,128)S(1)} %copy-done.3, f32[256,512]{1,0:T(8,128)S(1)} %collective-permute-done.21.refs_0_, f32[256,512]{1,0:T(8,128)S(1)} %collective-permute-done.22.refs_1_, f32[256,512]{1,0:T(8,128)S(1)} %collective-permute-done.23.refs_2_, f32[256,512]{1,0:T(8,128)S(1)} %collective-permute-done.24.refs_3_, ...), custom_call_target="tpu_custom_call" | custom-call | flops 2415919104 | bytes 1048576 | tf_op jit(solution)/shard_map/pallas_call | solution.py:359
  157.3 5.0 %collective-permute-done.26.up = f32[256,512]{1,0:T(8,128)S(1)} collective-permute-done((f32[256,512]{1,0:T(8,128)S(1)}, f32[256,512]{1,0:T(8,128)S(1)}, u32[]{:S(2)}, u32[]{:S(2)}) %collective-permute-start.26) | collective-permute-done | bytes 524320 | tf_op jit(solution)/shard_map/ppermute | solution.py:251
  162.3 3.6 %collective-permute-done.25.low = f32[256,512]{1,0:T(8,128)S(1)} collective-permute-done((f32[256,512]{1,0:T(8,128)S(1)}, f32[256,512]{1,0:T(8,128)S(1)}, u32[]{:S(2)}, u32[]{:S(2)}) %collective-permute-start.25) | collective-permute-done | bytes 524320 | tf_op jit(solution)/shard_map/ppermute | solution.py:251
  167.0 8.8 %collective-permute-start.27 = (f32[4,64,512]{2,1,0:T(8,128)S(1)}, f32[4,64,512]{2,1,0:T(8,128)S(1)}, u32[]{:S(2)}, u32[]{:S(2)}) collective-permute-start(f32[4,64,512]{2,1,0:T(8,128)S(1)} %slice_bitcast_fusion), channel_id=1, source_target_pairs={{0,32},{32,0},{1,33},{33,1},{2,34},{34,2},{3,35},{35,3},{4,36},{36... | collective-permute-start | bytes 1572872 | tf_op jit(solution)/shard_map/ppermute | solution.py:295
  181.7 4.3 %shard_map.58.near = f32[16,2048]{1,0:T(8,128)S(1)} custom-call(s32[4]{0:T(128)S(1)} %pad_add_fusion.idx, f32[256,512]{1,0:T(8,128)S(1)} %collective-permute-done.21.refs_0_, f32[256,512]{1,0:T(8,128)S(1)} %collective-permute-done.22.refs_1_, f32[256,512]{1,0:T(8,128)S(1)} %collective-permute-done.23.refs_2_, ...), custom_call_target="tpu_custom_call" | custom-call | flops 10000000 | bytes 1048576 | tf_op jit(solution)/shard_map/pallas_call | solution.py:365
  185.9 2.5 %shard_map.59 = f32[16,2048]{1,0:T(8,128)} custom-call(s32[4]{0:T(128)S(1)} %pad_add_fusion.idx, f32[16,2048]{1,0:T(8,128)S(1)} %shard_map.58.near, f32[256,512]{1,0:T(8,128)S(1)} %collective-permute-done.25.low, f32[256,512]{1,0:T(8,128)S(1)} %collective-permute-done.26.up), custom_call_target="tpu_custom_call" | custom-call | flops 10000000 | bytes 1048576 | tf_op jit(solution)/shard_map/pallas_call | solution.py:366
  (85 shorter events, 33.5 us)
Async XLA Ops:
  0.6 6.3 %collective-permute-start.2 = (f32[64,512]{1,0:T(8,128)}, f32[64,512]{1,0:T(8,128)S(1)}, u32[]{:S(2)}, u32[]{:S(2)}) collective-permute-start(f32[64,512]{1,0:T(8,128)} %bitcast.56), channel_id=1, source_target_pairs={{0,128},{64,192},{128,0},{192,64},{1,129},{65,193},{129,1},{193,65... | collective-permute-start | bytes 393224 | tf_op jit(solution)/shard_map/ppermute | solution.py:256
  4.3 7.5 %collective-permute-start.3 = (f32[64,512]{1,0:T(8,128)}, f32[64,512]{1,0:T(8,128)S(1)}, u32[]{:S(2)}, u32[]{:S(2)}) collective-permute-start(f32[64,512]{1,0:T(8,128)} %bitcast.57), channel_id=1, source_target_pairs={{0,64},{64,128},{128,192},{192,0},{1,65},{65,129},{129,193},{193,1... | collective-permute-start | bytes 393224 | tf_op jit(solution)/shard_map/ppermute | solution.py:256
  4.6 7.2 %collective-permute-start.1 = (f32[64,512]{1,0:T(8,128)}, f32[64,512]{1,0:T(8,128)S(1)}, u32[]{:S(2)}, u32[]{:S(2)}) collective-permute-start(f32[64,512]{1,0:T(8,128)} %bitcast.58), channel_id=1, source_target_pairs={{0,192},{64,0},{128,64},{192,128},{1,193},{65,1},{129,65},{193,129... | collective-permute-start | bytes 393224 | tf_op jit(solution)/shard_map/ppermute | solution.py:256
  12.8 6.0 %collective-permute-start.4 = (f32[4,64,512]{2,1,0:T(8,128)S(1)}, f32[4,64,512]{2,1,0:T(8,128)S(1)}, u32[]{:S(2)}, u32[]{:S(2)}) collective-permute-start(f32[4,64,512]{2,1,0:T(8,128)S(1)} %get-tuple-element.44), channel_id=1, source_target_pairs={{0,32},{32,0},{1,33},{33,1},{2,34},{34,2},{3,35},{35,3},{4,36},{36... | collective-permute-start | bytes 1572872 | tf_op jit(solution)/shard_map/ppermute | solution.py:295
  20.7 14.5 %collective-permute-start.5 = (f32[256,512]{1,0:T(8,128)S(1)}, f32[256,512]{1,0:T(8,128)S(1)}, u32[]{:S(2)}, u32[]{:S(2)}) collective-permute-start(f32[256,512]{1,0:T(8,128)S(1)} %get-tuple-element.24), channel_id=1, source_target_pairs={{0,1},{1,2},{2,3},{3,0},{4,5},{5,6},{6,7},{7,4},{8,9},{9,10},{10,1... | collective-permute-start | bytes 1572872 | tf_op jit(solution)/shard_map/ppermute | solution.py:251
  21.4 13.8 %collective-permute-start.6 = (f32[256,512]{1,0:T(8,128)S(1)}, f32[256,512]{1,0:T(8,128)S(1)}, u32[]{:S(2)}, u32[]{:S(2)}) collective-permute-start(f32[256,512]{1,0:T(8,128)S(1)} %get-tuple-element.25), channel_id=1, source_target_pairs={{0,3},{1,0},{2,1},{3,2},{4,7},{5,4},{6,5},{7,6},{8,11},{9,8},{10,9... | collective-permute-start | bytes 1572872 | tf_op jit(solution)/shard_map/ppermute | solution.py:251
  35.4 51.9 %collective-permute-start.7 = (f32[512,512]{1,0:T(8,128)S(1)}, f32[512,512]{1,0:T(8,128)S(1)}, u32[]{:S(2)}, u32[]{:S(2)}) collective-permute-start(f32[512,512]{1,0:T(8,128)S(1)} %get-tuple-element.26), channel_id=1, source_target_pairs={{0,1},{1,2},{2,3},{3,0},{4,5},{5,6},{6,7},{7,4},{8,9},{9,10},{10,1... | collective-permute-start | bytes 3145736 | tf_op jit(solution)/shard_map/ppermute | solution.py:251
  36.0 51.3 %collective-permute-start.8 = (f32[512,512]{1,0:T(8,128)S(1)}, f32[512,512]{1,0:T(8,128)S(1)}, u32[]{:S(2)}, u32[]{:S(2)}) collective-permute-start(f32[512,512]{1,0:T(8,128)S(1)} %get-tuple-element.27), channel_id=1, source_target_pairs={{0,3},{1,0},{2,1},{3,2},{4,7},{5,4},{6,5},{7,6},{8,11},{9,8},{10,9... | collective-permute-start | bytes 3145736 | tf_op jit(solution)/shard_map/ppermute | solution.py:251
  83.3 6.0 %collective-permute-start = (f32[512,256]{1,0:T(8,128)S(1)}, f32[512,256]{1,0:T(8,128)S(1)}, u32[]{:S(2)}, u32[]{:S(2)}) collective-permute-start(f32[512,256]{1,0:T(8,128)S(1)} %bitcast.50), channel_id=1, source_target_pairs={{0,32},{32,0},{1,33},{33,1},{2,34},{34,2},{3,35},{35,3},{4,36},{36... | collective-permute-start | bytes 1572872 | tf_op jit(solution)/shard_map/ppermute | solution.py:295
  87.7 7.9 %collective-permute-start.10 = (f32[128,512]{1,0:T(8,128)S(1)}, f32[128,512]{1,0:T(8,128)S(1)}, u32[]{:S(2)}, u32[]{:S(2)}) collective-permute-start(f32[128,512]{1,0:T(8,128)S(1)} %get-tuple-element.38), channel_id=1, source_target_pairs={{0,28},{4,0},{8,4},{12,8},{16,12},{20,16},{24,20},{28,24},{1,29},{... | collective-permute-start | bytes 786440 | tf_op jit(solution)/shard_map/ppermute | solution.py:251
  87.8 9.3 %collective-permute-start.9 = (f32[128,512]{1,0:T(8,128)S(1)}, f32[128,512]{1,0:T(8,128)S(1)}, u32[]{:S(2)}, u32[]{:S(2)}) collective-permute-start(f32[128,512]{1,0:T(8,128)S(1)} %get-tuple-element.39), channel_id=1, source_target_pairs={{0,4},{4,8},{8,12},{12,16},{16,20},{20,24},{24,28},{28,0},{1,5},{5... | collective-permute-start | bytes 786440 | tf_op jit(solution)/shard_map/ppermute | solution.py:251
  97.3 5.6 %collective-permute-start.11 = (f32[32,512]{1,0:T(8,128)S(1)}, f32[32,512]{1,0:T(8,128)S(1)}, u32[]{:S(2)}, u32[]{:S(2)}) collective-permute-start(f32[32,512]{1,0:T(8,128)S(1)} %get-tuple-element.49), channel_id=1, source_target_pairs={{0,8},{4,12},{8,16},{12,20},{16,24},{20,28},{24,0},{28,4},{1,9},{5... | collective-permute-start | bytes 196616 | tf_op jit(solution)/shard_map/ppermute | solution.py:251
  97.4 5.5 %collective-permute-start.12 = (f32[32,512]{1,0:T(8,128)S(1)}, f32[32,512]{1,0:T(8,128)S(1)}, u32[]{:S(2)}, u32[]{:S(2)}) collective-permute-start(f32[32,512]{1,0:T(8,128)S(1)} %get-tuple-element.45), channel_id=1, source_target_pairs={{0,24},{4,28},{8,0},{12,4},{16,8},{20,12},{24,16},{28,20},{1,25},{... | collective-permute-start | bytes 196616 | tf_op jit(solution)/shard_map/ppermute | solution.py:251
  102.9 9.4 %collective-permute-start.13 = (f32[64,512]{1,0:T(8,128)S(1)}, f32[64,512]{1,0:T(8,128)S(1)}, u32[]{:S(2)}, u32[]{:S(2)}) collective-permute-start(f32[64,512]{1,0:T(8,128)S(1)} %get-tuple-element.30), channel_id=1, source_target_pairs={{0,8},{4,12},{8,16},{12,20},{16,24},{20,28},{24,0},{28,4},{1,9},{5... | collective-permute-start | bytes 393224 | tf_op jit(solution)/shard_map/ppermute | solution.py:251
  104.9 7.4 %collective-permute-start.14 = (f32[64,512]{1,0:T(8,128)S(1)}, f32[64,512]{1,0:T(8,128)S(1)}, u32[]{:S(2)}, u32[]{:S(2)}) collective-permute-start(f32[64,512]{1,0:T(8,128)S(1)} %get-tuple-element.31), channel_id=1, source_target_pairs={{0,24},{4,28},{8,0},{12,4},{16,8},{20,12},{24,16},{28,20},{1,25},{... | collective-permute-start | bytes 393224 | tf_op jit(solution)/shard_map/ppermute | solution.py:251
  106.7 48.0 %copy-start.3 = (f32[2048,512]{1,0:T(8,128)S(1)}, f32[2048,512]{1,0:T(8,128)}, u32[]{:S(2)}) copy-start(f32[2048,512]{1,0:T(8,128)} %copy-done.1) | copy-start | bytes 12582916
  113.0 6.6 %collective-permute-start.15 = (f32[64,512]{1,0:T(8,128)S(1)}, f32[64,512]{1,0:T(8,128)S(1)}, u32[]{:S(2)}, u32[]{:S(2)}) collective-permute-start(f32[64,512]{1,0:T(8,128)S(1)} %shard_map.57), channel_id=1, source_target_pairs={{0,8},{4,12},{8,16},{12,20},{16,24},{20,28},{24,0},{28,4},{1,9},{5... | collective-permute-start | bytes 393224 | tf_op jit(solution)/shard_map/ppermute | solution.py:251
  114.3 5.3 %collective-permute-start.16 = (f32[64,512]{1,0:T(8,128)S(1)}, f32[64,512]{1,0:T(8,128)S(1)}, u32[]{:S(2)}, u32[]{:S(2)}) collective-permute-start(f32[64,512]{1,0:T(8,128)S(1)} %shard_map.57), channel_id=1, source_target_pairs={{0,24},{4,28},{8,0},{12,4},{16,8},{20,12},{24,16},{28,20},{1,25},{... | collective-permute-start | bytes 393224 | tf_op jit(solution)/shard_map/ppermute | solution.py:251
  119.7 6.0 %collective-permute-start.18 = (f32[32,512]{1,0:T(8,128)S(1)}, f32[32,512]{1,0:T(8,128)S(1)}, u32[]{:S(2)}, u32[]{:S(2)}) collective-permute-start(f32[32,512]{1,0:T(8,128)S(1)} %get-tuple-element.61), channel_id=1, source_target_pairs={{0,24},{4,28},{8,0},{12,4},{16,8},{20,12},{24,16},{28,20},{1,25},{... | collective-permute-start | bytes 196616 | tf_op jit(solution)/shard_map/ppermute | solution.py:251
  123.8 5.2 %collective-permute-start.17 = (f32[32,512]{1,0:T(8,128)S(1)}, f32[32,512]{1,0:T(8,128)S(1)}, u32[]{:S(2)}, u32[]{:S(2)}) collective-permute-start(f32[32,512]{1,0:T(8,128)S(1)} %slice.91), channel_id=1, source_target_pairs={{0,8},{4,12},{8,16},{12,20},{16,24},{20,28},{24,0},{28,4},{1,9},{5... | collective-permute-start | bytes 196616 | tf_op jit(solution)/shard_map/ppermute | solution.py:251
  129.1 5.6 %collective-permute-start.19 = (f32[128,512]{1,0:T(8,128)S(1)}, f32[128,512]{1,0:T(8,128)S(1)}, u32[]{:S(2)}, u32[]{:S(2)}) collective-permute-start(f32[128,512]{1,0:T(8,128)S(1)} %pad_maximum_fusion.2), channel_id=1, source_target_pairs={{0,28},{4,0},{8,4},{12,8},{16,12},{20,16},{24,20},{28,24},{1,29},{... | collective-permute-start | bytes 786440 | tf_op jit(solution)/shard_map/ppermute | solution.py:251
  129.2 7.2 %collective-permute-start.20 = (f32[128,512]{1,0:T(8,128)S(1)}, f32[128,512]{1,0:T(8,128)S(1)}, u32[]{:S(2)}, u32[]{:S(2)}) collective-permute-start(f32[128,512]{1,0:T(8,128)S(1)} %pad_maximum_fusion.3), channel_id=1, source_target_pairs={{0,4},{4,8},{8,12},{12,16},{16,20},{20,24},{24,28},{28,0},{1,5},{5... | collective-permute-start | bytes 786440 | tf_op jit(solution)/shard_map/ppermute | solution.py:251
  130.7 9.2 %collective-permute-start.22 = (f32[256,512]{1,0:T(8,128)S(1)}, f32[256,512]{1,0:T(8,128)S(1)}, u32[]{:S(2)}, u32[]{:S(2)}) collective-permute-start(f32[256,512]{1,0:T(8,128)S(1)} %get-tuple-element.53.refs_5_), channel_id=1, source_target_pairs={{0,3},{1,0},{2,1},{3,2},{4,7},{5,4},{6,5},{7,6},{8,11},{9,8},{10,9... | collective-permute-start | bytes 1572872 | tf_op jit(solution)/shard_map/ppermute | solution.py:251
  136.5 9.3 %collective-permute-start.23 = (f32[256,512]{1,0:T(8,128)S(1)}, f32[256,512]{1,0:T(8,128)S(1)}, u32[]{:S(2)}, u32[]{:S(2)}) collective-permute-start(f32[256,512]{1,0:T(8,128)S(1)} %constant_dynamic-update-slice_fusion.refs_4_), channel_id=1, source_target_pairs={{0,1},{1,2},{2,3},{3,0},{4,5},{5,6},{6,7},{7,4},{8,9},{9,10},{10,1... | collective-permute-start | bytes 1572872 | tf_op jit(solution)/shard_map/ppermute | solution.py:251
  137.3 17.4 %collective-permute-start.24 = (f32[256,512]{1,0:T(8,128)S(1)}, f32[256,512]{1,0:T(8,128)S(1)}, u32[]{:S(2)}, u32[]{:S(2)}) collective-permute-start(f32[256,512]{1,0:T(8,128)S(1)} %get-tuple-element.53.refs_5_), channel_id=1, source_target_pairs={{0,1},{1,2},{2,3},{3,0},{4,5},{5,6},{6,7},{7,4},{8,9},{9,10},{10,1... | collective-permute-start | bytes 1572872 | tf_op jit(solution)/shard_map/ppermute | solution.py:251
  137.5 17.2 %collective-permute-start.21 = (f32[256,512]{1,0:T(8,128)S(1)}, f32[256,512]{1,0:T(8,128)S(1)}, u32[]{:S(2)}, u32[]{:S(2)}) collective-permute-start(f32[256,512]{1,0:T(8,128)S(1)} %constant_dynamic-update-slice_fusion.refs_4_), channel_id=1, source_target_pairs={{0,3},{1,0},{2,1},{3,2},{4,7},{5,4},{6,5},{7,6},{8,11},{9,8},{10,9... | collective-permute-start | bytes 1572872 | tf_op jit(solution)/shard_map/ppermute | solution.py:251
  140.0 22.3 %collective-permute-start.26 = (f32[256,512]{1,0:T(8,128)S(1)}, f32[256,512]{1,0:T(8,128)S(1)}, u32[]{:S(2)}, u32[]{:S(2)}) collective-permute-start(f32[256,512]{1,0:T(8,128)S(1)} %collective-permute-done.22.refs_1_), channel_id=1, source_target_pairs={{0,3},{1,0},{2,1},{3,2},{4,7},{5,4},{6,5},{7,6},{8,11},{9,8},{10,9... | collective-permute-start | bytes 1572872 | tf_op jit(solution)/shard_map/ppermute | solution.py:251
  145.8 20.1 %collective-permute-start.25 = (f32[256,512]{1,0:T(8,128)S(1)}, f32[256,512]{1,0:T(8,128)S(1)}, u32[]{:S(2)}, u32[]{:S(2)}) collective-permute-start(f32[256,512]{1,0:T(8,128)S(1)} %collective-permute-done.23.refs_2_), channel_id=1, source_target_pairs={{0,1},{1,2},{2,3},{3,0},{4,5},{5,6},{6,7},{7,4},{8,9},{9,10},{10,1... | collective-permute-start | bytes 1572872 | tf_op jit(solution)/shard_map/ppermute | solution.py:251
  167.0 10.3 %collective-permute-start.27 = (f32[4,64,512]{2,1,0:T(8,128)S(1)}, f32[4,64,512]{2,1,0:T(8,128)S(1)}, u32[]{:S(2)}, u32[]{:S(2)}) collective-permute-start(f32[4,64,512]{2,1,0:T(8,128)S(1)} %slice_bitcast_fusion), channel_id=1, source_target_pairs={{0,32},{32,0},{1,33},{33,1},{2,34},{34,2},{3,35},{35,3},{4,36},{36... | collective-permute-start | bytes 1572872 | tf_op jit(solution)/shard_map/ppermute | solution.py:295
  177.4 11.0 %collective-permute-start.28 = (f32[64,512]{1,0:T(8,128)S(1)}, f32[64,512]{1,0:T(8,128)S(1)}, u32[]{:S(2)}, u32[]{:S(2)}) collective-permute-start(f32[64,512]{1,0:T(8,128)S(1)} %get-tuple-element.40), channel_id=1, source_target_pairs={{0,64},{64,128},{128,192},{192,0},{1,65},{65,129},{129,193},{193,1... | collective-permute-start | bytes 393224 | tf_op jit(solution)/shard_map/ppermute | solution.py:256
  179.3 9.2 %collective-permute-start.29 = (f32[64,512]{1,0:T(8,128)S(1)}, f32[64,512]{1,0:T(8,128)S(1)}, u32[]{:S(2)}, u32[]{:S(2)}) collective-permute-start(f32[64,512]{1,0:T(8,128)S(1)} %get-tuple-element.42), channel_id=1, source_target_pairs={{0,192},{64,0},{128,64},{192,128},{1,193},{65,1},{129,65},{193,129... | collective-permute-start | bytes 393224 | tf_op jit(solution)/shard_map/ppermute | solution.py:256
  180.6 7.8 %collective-permute-start.30 = (f32[64,512]{1,0:T(8,128)S(1)}, f32[64,512]{1,0:T(8,128)S(1)}, u32[]{:S(2)}, u32[]{:S(2)}) collective-permute-start(f32[64,512]{1,0:T(8,128)S(1)} %get-tuple-element.41), channel_id=1, source_target_pairs={{0,128},{64,192},{128,0},{192,64},{1,129},{65,193},{129,1},{193,65... | collective-permute-start | bytes 393224 | tf_op jit(solution)/shard_map/ppermute | solution.py:256
  (4 other events, 43.9 us)
